TPU v7x, 32 devices: a whole 2x2x4 slice. The times are simulated.
32 devices in a mesh: data: 32 (over z, y, x, core).
Axes of the slice: x: 2, y: 2, z: 4, core: 2. Of those that a mesh axis runs over, the one named last changes fastest.
Arguments:
- tokens: bfloat16 [16384, 384], P('data')
- w_in: bfloat16 [384, 1536], replicated
- w_out: bfloat16 [1536, 384], replicated
- task_heads: bfloat16 [3, 384, 13], replicated
- labels: int32 [3, 16384], P(None, 'data')
- label_mask: int32 [3, 16384], P(None, 'data')
Outputs:
- output 1: float32 [3], replicated
- output 2: float32 [589824], P('data')
- output 3: float32 [589824], P('data')
All inputs are finite; a program needn't handle non-finite values.
Results may differ from a plain program's by a relative error of at most 0.00270601.
Values are sent between devices in bfloat16 or wider.
A program may use at most 1 GiB of HBM per device.

v0:
```python
import jax
import jax.numpy as jnp
from jax import lax
from jax.sharding import PartitionSpec as P

SOLVER_STEPS = 20


def device_grads(x_loc, w_in, w_out, task_heads, lab_loc, mask_loc):
    pre_act = jnp.dot(x_loc, w_in, preferred_element_type=jnp.float32)
    act_out, gelu_slope = jax.jvp(jax.nn.gelu, (pre_act,), (jnp.ones_like(pre_act),))
    act_bf = act_out.astype(jnp.bfloat16)
    residual = x_loc.astype(jnp.float32) + jnp.dot(act_bf, w_out, preferred_element_type=jnp.float32)
    z_bf = residual.astype(jnp.bfloat16)
    logits = jnp.einsum("bd,tdc->tbc", z_bf, task_heads, preferred_element_type=jnp.float32)
    soft_prob = jax.nn.softmax(logits, axis=-1)
    class_ids = jnp.arange(logits.shape[-1])
    onehot = (lab_loc[:, :, None] == class_ids).astype(jnp.float32)
    d_logit = (mask_loc[:, :, None].astype(jnp.float32) * (soft_prob - onehot)).astype(jnp.bfloat16)
    d_resid = jnp.einsum("tbc,tdc->tbd", d_logit, task_heads, preferred_element_type=jnp.float32).astype(jnp.bfloat16)
    grad_w_out = jnp.einsum("bf,tbd->tfd", act_bf, d_resid, preferred_element_type=jnp.float32)
    d_act = jnp.einsum("tbd,fd->tbf", d_resid, w_out, preferred_element_type=jnp.float32)
    d_pre = (d_act * gelu_slope[None]).astype(jnp.bfloat16)
    grad_w_in = jnp.einsum("bd,tbf->tdf", x_loc, d_pre, preferred_element_type=jnp.float32)
    return grad_w_in, grad_w_out


def gram_of(grad_rows):
    return jnp.einsum("tk,sk->ts", grad_rows, grad_rows, precision=lax.Precision.HIGHEST, preferred_element_type=jnp.float32)


def solve_weights(gram_mat):
    num_tasks = gram_mat.shape[0]
    step_scale = jnp.trace(gram_mat) / num_tasks

    def solver_step(step_idx, weights):
        pull_vec = (gram_mat * weights[None, :]).sum(axis=1)
        raised = weights * jnp.exp(-pull_vec / step_scale)
        return raised / raised.sum()

    init_weights = jnp.full((num_tasks,), 1.0 / num_tasks, jnp.float32)
    return lax.fori_loop(0, SOLVER_STEPS, solver_step, init_weights)


def solution(mesh):
    group_size = mesh.shape["data"]

    def local_step(x_loc, w_in, w_out, task_heads, lab_loc, mask_loc):
        num_tasks = task_heads.shape[0]
        label_count = lax.psum(mask_loc.sum(axis=1), "data")
        inv_count = 1.0 / jnp.maximum(label_count, 1).astype(jnp.float32)
        grad_w_in, grad_w_out = device_grads(x_loc, w_in, w_out, task_heads, lab_loc, mask_loc)
        shards = []
        for grad_full in (grad_w_in, grad_w_out):
            scaled = (grad_full.reshape(num_tasks, group_size, -1) * inv_count[:, None, None]).astype(jnp.bfloat16)
            arrived = lax.all_to_all(scaled, "data", 1, 1, tiled=True)
            shards.append(arrived.sum(axis=1, dtype=jnp.float32))
        gram_mat = lax.psum(gram_of(shards[0]) + gram_of(shards[1]), "data")
        weights = solve_weights(gram_mat)
        grad_in = (weights[:, None] * shards[0]).sum(axis=0)
        grad_out = (weights[:, None] * shards[1]).sum(axis=0)
        return weights, grad_in, grad_out

    return jax.shard_map(local_step, mesh=mesh, in_specs=(P("data", None), P(), P(), P(), P(None, "data"), P(None, "data")), out_specs=(P(), P("data"), P("data")), check_vma=False)
```

profile of v0, /device:TPU:0, one launch (start us, length us, event | category | flops | bytes accessed | tf_op | source)
XLA Modules:
  0.0 410.3 jit_solution(5058773368658279055)
XLA Ops:
  0.6 0.9 fusion.32
  1.6 6.2 %fusion.11 = (f32[512,1536]{1,0:T(8,128)}, f32[512,1536]{1,0:T(8,128)}) fusion(bf16[512,384]{1,0:T(8,128)(2,1)} %param.8, bf16[384,1536]{1,0:T(8,128)(2,1)} %param.9), kind=kOutput, calls=%fused_computation.24 | convolution fusion | flops 616562688 | bytes 7864320 | tf_op jit(solution)/shard_map/dot_general | solution.py:10
  7.8 3.2 fusion.20
  11.7 7.0 %convolution_bitcast_fusion = f32[3,1536,384]{1,2,0:T(8,128)} fusion(bf16[3,512,384]{2,1,0:T(8,128)(2,1)S(1)} %convolution_convert_fusion, f32[512,1536]{1,0:T(8,128)} %get-tuple-element.58), kind=kOutput, calls=%fused_computation.11 | convolution fusion | flops 1819017216 | bytes 11403264 | tf_op jit(solution)/shard_map/bf,tbd->tfd/dot_general | solution.py:21
  18.6 8.1 %copy.25 = f32[3,1536,384]{2,1,0:T(8,128)} copy(f32[3,1536,384]{1,2,0:T(8,128)} %convolution_bitcast_fusion) | data formatting | bytes 14155776 | tf_op jit(solution)/shard_map/bf,tbd->tfd/transpose | solution.py:21
  26.8 7.6 %reshape.22 = f32[3,32,18432]{2,1,0:T(8,128)} reshape(f32[3,1536,384]{2,1,0:T(8,128)} %copy.25) | data formatting | bytes 14155776 | tf_op jit(solution)/shard_map/reshape | solution.py:55
  34.4 9.9 %convolution_bitcast_fusion.1 = f32[3,384,1536]{1,2,0:T(8,128)} fusion(bf16[3,512,384]{2,1,0:T(8,128)(2,1)S(1)} %convolution_convert_fusion, f32[512,1536]{1,0:T(8,128)} %get-tuple-element.57, bf16[1536,384]{1,0:T(8,128)(2,1)S(1)} %copy-done, bf16[512,384]{1,0:T(8,128)(2,1)S(1)} %copy-done.5), kind=kOutput, calls=%fused_computation.12 | convolution fusion | flops 3628597248 | bytes 12976128 | tf_op jit(solution)/shard_map/bd,tbf->tdf/dot_general | solution.py:24
  44.3 8.2 %copy.22 = f32[3,384,1536]{2,1,0:T(8,128)} copy(f32[3,384,1536]{1,2,0:T(8,128)} %convolution_bitcast_fusion.1) | data formatting | bytes 14155776 | tf_op jit(solution)/shard_map/bd,tbf->tdf/transpose | solution.py:24
  52.5 8.9 %reshape.21 = f32[3,32,18432]{2,1,0:T(8,128)} reshape(f32[3,384,1536]{2,1,0:T(8,128)} %copy.22) | data formatting | bytes 14155776 | tf_op jit(solution)/shard_map/reshape | solution.py:55
  61.5 41.9 %psum.14 = s32[3]{0:T(128)S(1)} all-reduce(s32[3]{0:T(128)S(1)} %get-tuple-element.53), channel_id=1, replica_groups=mesh['data'=32] {'data'}, use_global_device_ids=true, to_apply=%region_3.0 | all-reduce | flops 3 | bytes 24 | tf_op jit(solution)/shard_map/psum | solution.py:50
  103.4 7.7 %multiply_convert_fusion.1 = (bf16[3,32,18432]{2,1,0:T(8,128)(2,1)}, bf16[3,32,18432]{2,1,0:T(8,128)(2,1)S(1)}) fusion(f32[3,32,18432]{2,1,0:T(8,128)} %reshape.22, f32[3]{0:T(128)S(1)} %convert_divide_fusion, f32[3,32,18432]{2,1,0:T(8,128)} %reshape.21), kind=kLoop, calls=%fused_computation.9 | loop fusion | flops 7077888 | bytes 21233676 | tf_op jit(solution)/shard_map/convert_element_type | solution.py:55
  111.0 5.3 %copy.23 = bf16[3,32,18432]{2,0,1:T(4,128)(2,1)} copy(bf16[3,32,18432]{2,1,0:T(8,128)(2,1)S(1)} %get-tuple-element.56) | data formatting | bytes 7077888 | tf_op jit(solution)/shard_map/convert_element_type | solution.py:55
  116.3 4.8 %all-to-all-start = ((bf16[3,32,18432]{2,0,1:T(4,128)(2,1)}), bf16[3,32,18432]{2,0,1:T(4,128)(2,1)}, u32[]{:S(2)}, u32[]{:S(2)}) async-start(bf16[3,32,18432]{2,0,1:T(4,128)(2,1)} %copy.23), calls=%async_computation | async-start | bytes 9437184 | tf_op jit(solution)/shard_map/all_to_all | solution.py:56
  121.2 7.2 %copy.26 = bf16[3,32,18432]{2,0,1:T(4,128)(2,1)} copy(bf16[3,32,18432]{2,1,0:T(8,128)(2,1)} %get-tuple-element.55) | data formatting | bytes 7077888 | tf_op jit(solution)/shard_map/convert_element_type | solution.py:55
  128.4 95.0 %all-to-all-done = bf16[3,32,18432]{2,0,1:T(4,128)(2,1)} async-done(((bf16[3,32,18432]{2,0,1:T(4,128)(2,1)}), bf16[3,32,18432]{2,0,1:T(4,128)(2,1)}, u32[]{:S(2)}, u32[]{:S(2)}) %all-to-all-start) | async-done | bytes 3538976 | tf_op jit(solution)/shard_map/all_to_all | solution.py:56
  223.3 7.0 %all-to-all-start.1 = ((bf16[3,32,18432]{2,0,1:T(4,128)(2,1)}), bf16[3,32,18432]{2,0,1:T(4,128)(2,1)}, u32[]{:S(2)}, u32[]{:S(2)}) async-start(bf16[3,32,18432]{2,0,1:T(4,128)(2,1)} %copy.26), calls=%async_computation.1 | async-start | bytes 9437184 | tf_op jit(solution)/shard_map/all_to_all | solution.py:56
  230.3 4.5 %convert_reduce_fusion.1 = f32[3,18432]{1,0:T(4,128)S(1)} fusion(bf16[3,32,18432]{2,0,1:T(4,128)(2,1)} %all-to-all-done), kind=kLoop, calls=%fused_computation.7 | loop fusion | flops 3483648 | bytes 3760128 | tf_op jit(solution)/shard_map/reduce_sum | solution.py:57
  234.8 1.4 fusion.33
  236.2 94.8 %all-to-all-done.1 = bf16[3,32,18432]{2,0,1:T(4,128)(2,1)} async-done(((bf16[3,32,18432]{2,0,1:T(4,128)(2,1)}), bf16[3,32,18432]{2,0,1:T(4,128)(2,1)}, u32[]{:S(2)}, u32[]{:S(2)}) %all-to-all-start.1) | async-done | bytes 3538976 | tf_op jit(solution)/shard_map/all_to_all | solution.py:56
  331.1 4.5 %convert_reduce_fusion = f32[3,18432]{1,0:T(4,128)S(1)} fusion(bf16[3,32,18432]{2,0,1:T(4,128)(2,1)} %all-to-all-done.1), kind=kLoop, calls=%fused_computation.6 | loop fusion | flops 3483648 | bytes 3760128 | tf_op jit(solution)/shard_map/reduce_sum | solution.py:57
  335.5 1.4 convolution_add_fusion.1
  337.0 42.6 %psum.15 = f32[3,3]{1,0:T(4,128)S(1)} all-reduce(f32[3,3]{1,0:T(4,128)S(1)} %convolution_add_fusion.1), channel_id=1, replica_groups=mesh['data'=32] {'data'}, use_global_device_ids=true, to_apply=%region_6.0 | all-reduce | flops 9 | bytes 72 | tf_op jit(solution)/shard_map/psum | solution.py:58
  380.8 28.4 %while.11 = (s32[]{:T(128)}, f32[3]{0:T(128)S(1)}, f32[3,3]{1,0:T(4,128)S(1)}, f32[]{:T(128)}, s32[]{:T(128)}, /*index=5*/s32[]{:T(128)}) while((s32[]{:T(128)}, f32[3]{0:T(128)S(1)}, f32[3,3]{1,0:T(4,128)S(1)}, f32[]{:T(128)}, s32[]{:T(128)}, /*index=5*/s32[]{:T(128)}) %tuple.33), condition=%wide.region_11.12_spmd.clone, body=%wide.region_8.11_spmd.clone.sunk | while | flops 38 | bytes 236 | solution.py:42
  380.9 0.6 fusion.47
  381.6 0.6 broadcast_divide_fusion.2
  382.4 0.6 fusion.47
  383.0 0.6 broadcast_divide_fusion.2
  383.8 0.6 fusion.47
  384.4 0.6 broadcast_divide_fusion.2
  385.2 0.6 fusion.47
  385.8 0.6 broadcast_divide_fusion.2
  387.2 0.6 broadcast_divide_fusion.2
  388.7 0.6 broadcast_divide_fusion.2
  390.1 0.6 broadcast_divide_fusion.2
  391.5 0.6 broadcast_divide_fusion.2
  392.9 0.6 broadcast_divide_fusion.2
  394.3 0.6 broadcast_divide_fusion.2
  395.8 0.6 broadcast_divide_fusion.2
  397.2 0.6 broadcast_divide_fusion.2
  398.6 0.6 broadcast_divide_fusion.2
  400.0 0.6 broadcast_divide_fusion.2
  401.4 0.6 broadcast_divide_fusion.2
  402.9 0.6 broadcast_divide_fusion.2
  404.3 0.6 broadcast_divide_fusion.2
  405.7 0.6 broadcast_divide_fusion.2
  407.1 0.6 broadcast_divide_fusion.2
  408.5 0.6 broadcast_divide_fusion.2
  409.2 1.1 multiply_reduce_fusion.1
  (72 shorter events, 13.5 us)
Async XLA Ops:
  0.6 7.2 %copy-start = (bf16[1536,384]{1,0:T(8,128)(2,1)S(1)}, bf16[1536,384]{1,0:T(8,128)(2,1)}, u32[]{:S(2)}) copy-start(bf16[1536,384]{1,0:T(8,128)(2,1)} %param.10) | copy-start | bytes 3538948
  1.6 6.2 %copy-start.2 = (bf16[3,384,13]{1,2,0:T(8,128)(2,1)S(1)}, bf16[3,384,13]{1,2,0:T(8,128)(2,1)}, u32[]{:S(2)}) copy-start(bf16[3,384,13]{1,2,0:T(8,128)(2,1)} %param.11) | copy-start | bytes 89860
  1.6 6.2 %copy-start.5 = (bf16[512,384]{1,0:T(8,128)(2,1)S(1)}, bf16[512,384]{1,0:T(8,128)(2,1)}, u32[]{:S(2)}) copy-start(bf16[512,384]{1,0:T(8,128)(2,1)} %param.8) | copy-start | bytes 1179652
  7.8 3.3 copy-start.4
  116.3 107.0 %all-to-all-start = ((bf16[3,32,18432]{2,0,1:T(4,128)(2,1)}), bf16[3,32,18432]{2,0,1:T(4,128)(2,1)}, u32[]{:S(2)}, u32[]{:S(2)}) async-start(bf16[3,32,18432]{2,0,1:T(4,128)(2,1)} %copy.23), calls=%async_computation | async-start | bytes 9437184 | tf_op jit(solution)/shard_map/all_to_all | solution.py:56
  223.3 107.7 %all-to-all-start.1 = ((bf16[3,32,18432]{2,0,1:T(4,128)(2,1)}), bf16[3,32,18432]{2,0,1:T(4,128)(2,1)}, u32[]{:S(2)}, u32[]{:S(2)}) async-start(bf16[3,32,18432]{2,0,1:T(4,128)(2,1)} %copy.26), calls=%async_computation.1 | async-start | bytes 9437184 | tf_op jit(solution)/shard_map/all_to_all | solution.py:56
  234.8 175.5 %copy-start.1 = (bf16[1536,384]{1,0:T(8,128)(2,1)S(1)}, bf16[1536,384]{1,0:T(8,128)(2,1)}, u32[]{:S(2)}) copy-start(bf16[1536,384]{1,0:T(8,128)(2,1)} %param.10) | copy-start | bytes 3538948
  409.2 1.1 copy-start.3
where the time goes:
time: 412 us; the launch traced here: 410 us
  waiting for transfers between devices  190 us (46%)
  blocking collectives  84.5 us (21%)
  other arithmetic  46.9 us (11%)
  local copies, waits for them, and re-layouts  45.4 us (11%)
  matrix products  29.7 us (7%)
  starting transfers between devices  11.8 us (3%)
    all_to_all x2, waiting for transfers between devices, local_step(): arrived = lax.all_to_all(scaled, 'data', 1, 1, tiled=True)  190 us
    psum x1, blocking collectives, local_step(): gram_mat = lax.psum(gram_of(shards[0]) + gram_of(shards[1]), 'data')  42.6 us
    psum x1, blocking collectives, local_step(): label_count = lax.psum(mask_loc.sum(axis=1), 'data')  41.9 us
    reshape x2, local copies, waits for them, and re-layouts, local_step(): grad_full.reshape(num_tasks, group_size, -1) * inv_count[:, None, None]  16.5 us
    div x20, other arithmetic, solver_step(): return raised / raised.sum()  13 us
    convert_element_type x2, local copies, waits for them, and re-layouts, local_step(): (grad_full.reshape(num_tasks, group_size, -1) * inv_count[:, None, None])...  12.5 us
    reduce_sum x20, other arithmetic, solver_step(): return raised / raised.sum()  12.4 us
    all_to_all x2, starting transfers between devices, local_step(): arrived = lax.all_to_all(scaled, 'data', 1, 1, tiled=True)  11.8 us
  transfers between devices with their start and end apart: 2, of which 2 were waited for; matrix products, arithmetic and copies ran while one was open for 3% of the time, Pallas kernels for 0%

commit v1 on v0

v1 whole, which is shorter than its diff:
```python
import jax
import jax.numpy as jnp
from jax import lax
from jax.experimental import pallas as pl
from jax.experimental.pallas import tpu as pltpu
from jax.sharding import PartitionSpec as P

MESH = pl.DeviceIdType.MESH
SOLVER_STEPS = 20
N_DEV = 32
TOK, DIM, HID, TASKS, CLS, PAD = 512, 384, 1536, 3, 13, 16
ZA, ZB = 16, 8
CHUNKS = 4
ROWS = DIM // CHUNKS
GELU_C = 0.7978845608028654
GELU_A = 0.044715
N_SEM = 48

F32, BF16 = jnp.float32, jnp.bfloat16


def dot(a, b):
    return jnp.dot(a, b, preferred_element_type=F32)


def dot_nt(a, b):
    return lax.dot_general(a, b, (((1,), (1,)), ((), ())), preferred_element_type=F32)


def gelu_cdf(p):
    sq = p * p
    t = jnp.tanh(GELU_C * (p + GELU_A * (sq * p)))
    return sq, t, 0.5 * (1.0 + t)


def kernel(x_ref, w1_ref, w2_ref, hp_ref, lab_ref, msk_ref, al_ref, o1_ref, o2_ref,
           cnts, grams, gx, ge, ht, w1s, w2s, a_own, a_t, gp, dz, qt, inv, acc1, acc2,
           rc1, rc2, ra1, ra2, rb1, rb2, g1s, g2s, sb, rb,
           ss, rs, cs, cr, gs, gr):
    me = lax.axis_index("data")
    c = lax.rem(me, 2)
    x = lax.rem(me // 2, 2)
    y = lax.rem(me // 4, 2)
    za = lax.rem(me // ZA, 2)
    zb = lax.rem(me // ZB, 2)
    to_c = me + (1 - 2 * c)
    to_x = me + 2 * (1 - 2 * x)
    to_y = me + 4 * (1 - 2 * y)
    to_za = me + ZA * (1 - 2 * za)
    to_zb = me + ZB * (1 - 2 * zb)

    used = []

    def rcopy(src, dst, dev):
        i = len(used)
        used.append(i)
        return pltpu.make_async_remote_copy(src_ref=src, dst_ref=dst, send_sem=ss.at[i], recv_sem=rs.at[i],
                                            device_id=(dev,), device_id_type=MESH)

    pending = []

    def start(cp):
        cp.start()
        pending.append(cp)
        return cp

    def row_copy(buf, src_row, send_sem, recv_sem, dev):
        return pltpu.make_async_remote_copy(src_ref=buf.at[src_row], dst_ref=buf.at[src_row], send_sem=send_sem,
                                            recv_sem=recv_sem, device_id=(dev,), device_id_type=MESH)

    def exchange_start(buf, s_sem, r_sem):
        def go(i, _):
            row_copy(buf, me, s_sem.at[i], r_sem.at[me], lax.rem(me + i, N_DEV)).start()
            return 0
        lax.fori_loop(1, N_DEV, go, 0)

    def exchange_wait(buf, s_sem, r_sem):
        def go(i, _):
            peer = lax.rem(me + i, N_DEV)
            row_copy(buf, me, s_sem.at[i], r_sem.at[me], peer).wait_send()
            row_copy(buf, peer, s_sem.at[i], r_sem.at[peer], peer).wait_recv()
            return 0
        lax.fori_loop(1, N_DEV, go, 0)

    bar = pltpu.get_barrier_semaphore()

    def sig(i, _):
        pl.semaphore_signal(bar, inc=1, device_id=(lax.rem(me + i, N_DEV),), device_id_type=MESH)
        return 0
    lax.fori_loop(1, N_DEV, sig, 0)

    col = lax.broadcasted_iota(jnp.int32, (DIM, 1), 0)
    blk = (col * 43691) >> 19
    off = col - 12 * blk
    dev = (((blk >> 4) & 1) + 4 * ((blk >> 3) & 1) + ZB * ((blk >> 2) & 1) + ZA * ((blk >> 1) & 1) + 2 * (blk & 1))
    perm = (lax.broadcasted_iota(jnp.int32, (DIM, DIM), 1) == 12 * dev + off).astype(BF16)
    gx[0] = dot_nt(perm, x_ref[...]).astype(BF16)
    lane = lax.broadcasted_iota(jnp.int32, (1, 128), 1)
    row = jnp.zeros((1, 128), F32)
    for t in range(TASKS):
        row = row + jnp.where(lane == t, jnp.sum(msk_ref[t:t + 1, :].astype(F32), axis=1, keepdims=True), 0.0)
    cnts[me] = row

    pl.semaphore_wait(bar, N_DEV - 1)

    def chunk(k):
        return pl.ds(k * ROWS, ROWS)
    to_2 = [start(rcopy(gx.at[0, chunk(k)], gx.at[2, chunk(k)], to_za)) for k in range(CHUNKS)]
    to_1 = [start(rcopy(gx.at[0, chunk(k)], gx.at[1, chunk(k)], to_x)) for k in range(CHUNKS)]
    exchange_start(cnts, cs, cr)
    to_3 = [rcopy(gx.at[2, chunk(k)], gx.at[3, chunk(k)], to_x) for k in range(CHUNKS)]
    e_2 = rcopy(ge.at[0], ge.at[2], to_za)
    e_1 = rcopy(ge.at[0], ge.at[1], to_x)
    e_3 = rcopy(ge.at[2], ge.at[3], to_x)

    def fwd(i, _):
        cols = pl.ds(pl.multiple_of(i * 256, 256), 256)
        p = dot(x_ref[...], w1_ref[:, cols])
        a_own[:, cols] = (p * gelu_cdf(p)[2]).astype(BF16)
        return 0
    lax.fori_loop(0, HID // 256, fwd, 0)
    z = (x_ref[...].astype(F32) + dot(a_own[...], w2_ref[...])).astype(BF16)
    logits = dot_nt(hp_ref[...], z)
    cls = lax.broadcasted_iota(jnp.int32, (PAD, TOK), 0)
    valid = cls < CLS
    for t in range(TASKS):
        lg = jnp.where(valid, logits[PAD * t:PAD * (t + 1)], -jnp.inf)
        ex = jnp.exp(lg - jnp.max(lg, axis=0, keepdims=True))
        sm = ex / jnp.sum(ex, axis=0, keepdims=True)
        hot = (lab_ref[t:t + 1, :] == cls).astype(F32)
        ge[0, t] = jnp.where(valid, msk_ref[t:t + 1, :].astype(F32) * (sm - hot), 0.0).astype(BF16)
    start(e_2)
    start(e_1)

    seg = (col * 43691) >> 21
    src = 48 * (((seg >> 2) & 1) + ZB * ((seg >> 1) & 1) + 4 * (seg & 1) + ZA * za + 2 * x) + (col - 48 * seg)
    sel = (lax.broadcasted_iota(jnp.int32, (DIM, HID), 1) == src).astype(BF16)
    w1_rows = dot_nt(sel, w1_ref[...]).astype(BF16)
    w1s[...] = dot_nt(w1_rows, perm).astype(BF16)
    for k in range(8):
        dv = ((k >> 2) & 1) + ZB * ((k >> 1) & 1) + 4 * (k & 1) + ZA * za + 2 * x
        w2s[48 * k:48 * (k + 1), :] = w2_ref[pl.ds(pl.multiple_of(48 * dv, 16), 48), :]
    for t in range(TASKS):
        ht[t] = jnp.transpose(hp_ref[PAD * t:PAD * (t + 1), :].astype(F32)).astype(BF16)

    def acts(s):
        for r in range(3):
            rows = slice(128 * r, 128 * (r + 1))
            p = dot(w1s[rows, :], gx[s])
            sq, t, cdf = gelu_cdf(p)
            a_t[rows, :] = (p * cdf).astype(BF16)
            gp[rows, :] = cdf + (0.5 * GELU_C) * p * (1.0 - t * t) * (1.0 + (3.0 * GELU_A) * sq)

    def grads(s, t, first):
        dz[...] = dot(ht[t], ge[s, t]).astype(BF16)
        for r in range(3):
            rows = slice(128 * r, 128 * (r + 1))
            qt[rows, :] = (dot(w2s[rows, :], dz[...]) * gp[rows, :]).astype(BF16)
        sc = inv[t]
        d1 = (dot_nt(gx[s], qt[...]) * sc).astype(BF16).astype(F32)
        acc1[t] = d1 if first else acc1[t] + d1
        d2 = (dot_nt(a_t[...], dz[...]) * sc).astype(BF16).astype(F32)
        acc2[t] = d2 if first else acc2[t] + d2

    acts(0)
    to_2[0].wait_recv()
    start(to_3[0])
    exchange_wait(cnts, cs, cr)
    total = jnp.sum(cnts[...], axis=0)
    recip = 1.0 / jnp.maximum(total, 1.0)
    for t in range(TASKS):
        inv[t] = jnp.broadcast_to(recip[:, t:t + 1], (1, DIM))
    for t in range(TASKS):
        grads(0, t, True)
    to_2[1].wait_recv()
    start(to_3[1])
    for cp in to_1:
        cp.wait_recv()
    acts(1)
    e_1.wait_recv()
    to_2[2].wait_recv()
    start(to_3[2])
    for t in range(TASKS):
        grads(1, t, False)
    to_2[3].wait_recv()
    start(to_3[3])
    e_2.wait_recv()
    start(e_3)
    acts(2)
    for t in range(TASKS):
        grads(2, t, False)
    for cp in to_3:
        cp.wait_recv()
    acts(3)
    e_3.wait_recv()

    def rows_of(base, n):
        return pl.ds(pl.multiple_of(base, 48), n)
    c1, c2 = [], []
    for t in range(TASKS):
        grads(3, t, False)
        c1.append(start(rcopy(acc1.at[t, rows_of(192 * (1 - c), 192)], rc1.at[t], to_c)))
        c2.append(start(rcopy(acc2.at[t, rows_of(192 * (1 - c), 192)], rc2.at[t], to_c)))
    b0 = 192 * c
    h1, h2 = [], []
    for t in range(TASKS):
        c1[t].wait_recv()
        mine = rows_of(b0, 192)
        acc1[t, mine] = acc1[t, mine] + rc1[t]
        h1.append(start(rcopy(acc1.at[t, rows_of(b0 + 96 * (1 - y), 96)], ra1.at[t], to_y)))
        c2[t].wait_recv()
        acc2[t, mine] = acc2[t, mine] + rc2[t]
        h2.append(start(rcopy(acc2.at[t, rows_of(b0 + 96 * (1 - zb), 96)], ra2.at[t], to_zb)))
    q1, q2 = [], []
    for t in range(TASKS):
        h1[t].wait_recv()
        mine = rows_of(b0 + 96 * y, 96)
        acc1[t, mine] = acc1[t, mine] + ra1[t]
        q1.append(start(rcopy(acc1.at[t, rows_of(b0 + 96 * y + 48 * (1 - zb), 48)], rb1.at[t], to_zb)))
        h2[t].wait_recv()
        mine = rows_of(b0 + 96 * zb, 96)
        acc2[t, mine] = acc2[t, mine] + ra2[t]
        q2.append(start(rcopy(acc2.at[t, rows_of(b0 + 96 * zb + 48 * (1 - y), 48)], rb2.at[t], to_y)))
    own = 2 * za + x
    zero4 = jnp.zeros((4, DIM), F32)
    for t in range(TASKS):
        q1[t].wait_recv()
        g = acc1[t, rows_of(b0 + 96 * y + 48 * zb, 48)] + rb1[t]
        g1s[t] = g
        for k in range(4):
            sb[k, t] = jnp.concatenate([g[12 * k:12 * (k + 1)], zero4], axis=0)
        q2[t].wait_recv()
        g2s[t] = acc2[t, rows_of(b0 + 96 * zb + 48 * y, 48)] + rb2[t]

    row = jnp.zeros((1, 128), F32)
    pairs = [(0, 0), (0, 1), (0, 2), (1, 1), (1, 2), (2, 2)]
    for i, (t, s) in enumerate(pairs):
        part = jnp.sum(g1s[t] * g1s[s] + g2s[t] * g2s[s], axis=0, keepdims=True)
        row = row + jnp.where(lane == i, jnp.sum(part, axis=1, keepdims=True), 0.0)
    grams[me] = row
    exchange_start(grams, gs, gr)
    fx, fz = 1 - 2 * x, 2 * (1 - 2 * za)
    back = []
    for dk, to in ((fx, to_x), (fz, to_za), (fx + fz, to_x + to_za - me)):
        back.append(start(rcopy(sb.at[own + dk], rb.at[own], to)))
    rb[own] = sb[own]
    exchange_wait(grams, gs, gr)
    m = jnp.sum(grams[...], axis=0)
    ent = [m[:, i:i + 1] for i in range(6)]
    gram = {}
    for i, (t, s) in enumerate(pairs):
        gram[t, s] = gram[s, t] = ent[i]
    scale = (ent[0] + ent[3] + ent[5]) / TASKS

    def solve(_, w):
        up = []
        for t in range(TASKS):
            pull = gram[t, 0] * w[0] + gram[t, 1] * w[1] + gram[t, 2] * w[2]
            up.append(w[t] * jnp.exp(-pull / scale))
        tot = up[0] + up[1] + up[2]
        return tuple(u / tot for u in up)
    first = jnp.full((1, 1), 1.0 / TASKS, F32)
    w = lax.fori_loop(0, SOLVER_STEPS, solve, (first, first, first))
    al_ref[...] = jnp.concatenate(w, axis=1)
    gg = w[0] * g2s[0] + w[1] * g2s[1] + w[2] * g2s[2]
    for k in range(3):
        o2_ref[pl.ds(k, 48, stride=3), :] = gg[:, 128 * k:128 * (k + 1)]
    for cp in back:
        cp.wait_recv()
    for k in range(4):
        o1_ref[k] = w[0] * rb[k, 0] + w[1] * rb[k, 1] + w[2] * rb[k, 2]
    for cp in pending:
        cp.wait_send()


def solution(mesh):
    def step(tokens, w_in, w_out, heads, lab, msk):
        hp = jnp.pad(heads.transpose(0, 2, 1), ((0, 0), (0, PAD - CLS), (0, 0))).reshape(TASKS * PAD, DIM)
        vm = pl.BlockSpec(memory_space=pltpu.VMEM)
        dma = pltpu.SemaphoreType.DMA
        alpha, o1, o2 = pl.pallas_call(
            kernel,
            name="step",
            out_shape=(jax.ShapeDtypeStruct((1, TASKS), F32), jax.ShapeDtypeStruct((4, 16, DIM), F32),
                       jax.ShapeDtypeStruct((144, 128), F32)),
            in_specs=[vm] * 6,
            out_specs=(vm, vm, vm),
            scratch_shapes=[
                pltpu.VMEM((N_DEV, 1, 128), F32), pltpu.VMEM((N_DEV, 1, 128), F32),
                pltpu.VMEM((4, DIM, TOK), BF16), pltpu.VMEM((4, TASKS, PAD, TOK), BF16),
                pltpu.VMEM((TASKS, DIM, PAD), BF16), pltpu.VMEM((DIM, DIM), BF16), pltpu.VMEM((DIM, DIM), BF16),
                pltpu.VMEM((TOK, HID), BF16), pltpu.VMEM((DIM, TOK), BF16), pltpu.VMEM((DIM, TOK), F32),
                pltpu.VMEM((DIM, TOK), BF16), pltpu.VMEM((DIM, TOK), BF16), pltpu.VMEM((TASKS, 1, DIM), F32),
                pltpu.VMEM((TASKS, DIM, DIM), F32), pltpu.VMEM((TASKS, DIM, DIM), F32),
                pltpu.VMEM((TASKS, 192, DIM), F32), pltpu.VMEM((TASKS, 192, DIM), F32),
                pltpu.VMEM((TASKS, 96, DIM), F32), pltpu.VMEM((TASKS, 96, DIM), F32),
                pltpu.VMEM((TASKS, 48, DIM), F32), pltpu.VMEM((TASKS, 48, DIM), F32),
                pltpu.VMEM((TASKS, 48, DIM), F32), pltpu.VMEM((TASKS, 48, DIM), F32),
                pltpu.VMEM((4, TASKS, 16, DIM), F32), pltpu.VMEM((4, TASKS, 16, DIM), F32),
                dma((N_SEM,)), dma((N_SEM,)), dma((N_DEV,)), dma((N_DEV,)), dma((N_DEV,)), dma((N_DEV,)),
            ],
            compiler_params=pltpu.CompilerParams(collective_id=0, has_side_effects=True, vmem_limit_bytes=56 * 2**20),
        )(tokens, w_in, w_out, hp, lab, msk)
        g = o1[:, :12].reshape(2, 2, 12, 2, 2, 2, 48).transpose(2, 0, 4, 5, 1, 3, 6).reshape(-1)
        return alpha.reshape(TASKS), g, o2.reshape(-1)

    return jax.shard_map(step, mesh=mesh, in_specs=(P("data", None), P(), P(), P(), P(None, "data"), P(None, "data")),
                         out_specs=(P(), P("data"), P("data")), check_vma=False)
```

time: 412 us -> 83 us (0.20)
  waiting for transfers between devices: 190 us -> 0 us
  blocking collectives: 84.5 us -> 0 us
  Pallas kernels: 0 us -> 75.5 us
  other arithmetic: 46.9 us -> 0 us
  local copies, waits for them, and re-layouts: 45.4 us -> 6.38 us
  matrix products: 29.7 us -> 0 us
  starting transfers between devices: 11.8 us -> 0 us
    all_to_all x2 -> x0, waiting for transfers between devices: 190 us -> none  [local_step(): arrived = lax.all_to_all(scaled, 'data', 1, 1, tiled=True)]
    psum x2 -> x0, blocking collectives: 84.5 us -> none  [the longest x1 42.6 us: local_step(): gram_mat = lax.psum(gram_of(shards[0]) + gram_of(shards[1]), 'data')]
    pallas_call x0 -> x1, Pallas kernels: none -> 75.5 us  [step(): pl.pallas_call(kernel, name='step', out_shape=(jax.ShapeDtypeStruct((1, T...]
    dot_general x7 -> x0, matrix products: 29.7 us -> none  [the longest x1 9.94 us: device_grads(): jnp.einsum('bd,tbf->tdf', x_loc, d_pre, preferred_element_type=jnp.float32)]
    reduce_sum x45 -> x0, other arithmetic: 26.2 us -> none  [the longest x20 12.4 us: solver_step(): return raised / raised.sum()]
    transpose x2 -> x1, local copies, waits for them, and re-layouts: 16.4 us -> 0.1 us  [step(): o1[:, :12].reshape(2, 2, 12, 2, 2, 2, 48).transpose(2, 0, 4, 5, 1, 3, 6)]
    reshape x2, local copies, waits for them, and re-layouts: 16.5 us -> 1.26 us  [step(): o1[:, :12].reshape(2, 2, 12, 2, 2, 2, 48).transpose(2, 0, 4, 5, 1, 3, 6)]
    div x21 -> x0, other arithmetic: 13 us -> none  [the longest x20 13 us: solver_step(): return raised / raised.sum()]
  transfers between devices with their start and end apart: 2 -> 0, of which waited for: 2 -> 0; matrix products, arithmetic and copies ran while one was open for 3% -> 0% of each run, Pallas kernels for 0% -> 0%
where the time goes in v1:
time: 83 us; the launch traced here: 82.5 us
  Pallas kernels  75.5 us (91%)
  local copies, waits for them, and re-layouts  6.38 us (8%)
    pallas_call x1, Pallas kernels, step(): pl.pallas_call(kernel, name='step', out_shape=(jax.ShapeDtypeStruct((1, T...  75.5 us
    unnamed x2, local copies, waits for them, and re-layouts  2.7 us

profile of v1, /device:TPU:0, one launch (start us, length us, event | category | flops | bytes accessed | tf_op | source)
XLA Modules:
  0.0 82.5 jit_solution(14044200209694369836)
XLA Ops:
  0.6 1.4 %pad.4 = bf16[3,16,384]{2,1,0:T(8,128)(2,1)} pad(bf16[3,13,384]{2,1,0:T(8,128)(2,1)} %bitcast.12, bf16[]{:T(256)} %constant.2.clone.1), padding=0_0x0_3x0_0 | pad | bytes 66818 | tf_op jit(solution)/shard_map/jit(_pad)/pad | solution.py:278
  2.0 75.5 %step.1 = (f32[1,3]{1,0:T(1,128)}, f32[4,16,384]{2,1,0:T(8,128)}, f32[144,128]{1,0:T(8,128)}) custom-call(bf16[512,384]{1,0:T(8,128)(2,1)} %x_ref.1, bf16[384,1536]{1,0:T(8,128)(2,1)} %w1_ref.1, bf16[1536,384]{1,0:T(8,128)(2,1)} %w2_ref.1, bf16[48,384]{1,0:T(8,128)(2,1)} %bitcast.9, s32[3,512]{1,0:T(4,128)} %lab_ref.1, s32[3,512]{1,0:T(4,128)} %msk_ref.1), custom_call_target="tpu_custom_call" | custom-call | tf_op jit(solution)/shard_map/step/pallas_call | solution.py:281
  77.5 0.9 %copy.9 = f32[4,12,384]{2,0,1:T(4,128)S(1)} copy(f32[4,12,384]{2,1,0:T(8,128)} %bitcast.10) | data formatting | bytes 147456 | tf_op jit(solution)/shard_map/slice | solution.py:304
  78.4 0.3 reshape.23
  78.8 0.1 copy.10
  78.9 0.9 %reshape.24 = f32[18432]{0:T(1024)} reshape(f32[12,2,2,2,2,2,48]{6,5,4,3,2,1,0:T(2,128)S(1)} %copy.10) | data formatting | bytes 147456 | tf_op jit(solution)/shard_map/reshape | solution.py:304
  79.8 1.2 %copy.13 = f32[3]{0:T(128)} copy(f32[3]{0:T(128)} %bitcast.13) | data formatting | bytes 24
  81.0 1.5 %copy.14 = f32[18432]{0:T(1024)} copy(f32[18432]{0:T(1024)} %bitcast.11) | data formatting | bytes 147456

commit v2 on v1

--- a/solution.py
+++ b/solution.py
@@ -33,10 +33,10 @@
     return sq, t, 0.5 * (1.0 + t)
 
 
-def kernel(x_ref, w1_ref, w2_ref, hp_ref, lab_ref, msk_ref, al_ref, o1_ref, o2_ref,
-           cnts, grams, gx, ge, ht, w1s, w2s, a_own, a_t, gp, dz, qt, inv, acc1, acc2,
+def kernel(x_hbm, w1_hbm, w2_hbm, h_hbm, lab_hbm, msk_hbm, al_ref, o1_ref, o2_ref,
+           x_ref, w1_ref, w2_ref, h_ref, lab_ref, msk_ref, hp_ref, cnts, grams, gx, ge, ht, w1s, w2s, a_own, a_t, gp, dz, qt, inv, acc1, acc2,
            rc1, rc2, ra1, ra2, rb1, rb2, g1s, g2s, sb, rb,
-           ss, rs, cs, cr, gs, gr):
+           ss, rs, cs, cr, gs, gr, ls):
     me = lax.axis_index("data")
     c = lax.rem(me, 2)
     x = lax.rem(me // 2, 2)
@@ -82,6 +82,11 @@
             return 0
         lax.fori_loop(1, N_DEV, go, 0)
 
+    loads = [pltpu.make_async_copy(a, b, ls.at[i]) for i, (a, b) in enumerate((
+        (x_hbm, x_ref), (msk_hbm, msk_ref), (w1_hbm, w1_ref), (w2_hbm, w2_ref), (h_hbm, h_ref), (lab_hbm, lab_ref)))]
+    for cp in loads:
+        cp.start()
+
     bar = pltpu.get_barrier_semaphore()
 
     def sig(i, _):
@@ -94,9 +99,11 @@
     off = col - 12 * blk
     dev = (((blk >> 4) & 1) + 4 * ((blk >> 3) & 1) + ZB * ((blk >> 2) & 1) + ZA * ((blk >> 1) & 1) + 2 * (blk & 1))
     perm = (lax.broadcasted_iota(jnp.int32, (DIM, DIM), 1) == 12 * dev + off).astype(BF16)
+    loads[0].wait()
     gx[0] = dot_nt(perm, x_ref[...]).astype(BF16)
     lane = lax.broadcasted_iota(jnp.int32, (1, 128), 1)
     row = jnp.zeros((1, 128), F32)
+    loads[1].wait()
     for t in range(TASKS):
         row = row + jnp.where(lane == t, jnp.sum(msk_ref[t:t + 1, :].astype(F32), axis=1, keepdims=True), 0.0)
     cnts[me] = row
@@ -105,14 +112,19 @@
 
     def chunk(k):
         return pl.ds(k * ROWS, ROWS)
+    exchange_start(cnts, cs, cr)
     to_2 = [start(rcopy(gx.at[0, chunk(k)], gx.at[2, chunk(k)], to_za)) for k in range(CHUNKS)]
     to_1 = [start(rcopy(gx.at[0, chunk(k)], gx.at[1, chunk(k)], to_x)) for k in range(CHUNKS)]
-    exchange_start(cnts, cs, cr)
     to_3 = [rcopy(gx.at[2, chunk(k)], gx.at[3, chunk(k)], to_x) for k in range(CHUNKS)]
     e_2 = rcopy(ge.at[0], ge.at[2], to_za)
     e_1 = rcopy(ge.at[0], ge.at[1], to_x)
     e_3 = rcopy(ge.at[2], ge.at[3], to_x)
 
+    for cp in loads[2:]:
+        cp.wait()
+    hp_ref[...] = jnp.zeros_like(hp_ref)
+    for t in range(TASKS):
+        hp_ref[PAD * t:PAD * t + CLS, :] = h_ref[t]
     def fwd(i, _):
         cols = pl.ds(pl.multiple_of(i * 256, 256), 256)
         p = dot(x_ref[...], w1_ref[:, cols])
@@ -163,8 +175,6 @@
         acc2[t] = d2 if first else acc2[t] + d2
 
     acts(0)
-    to_2[0].wait_recv()
-    start(to_3[0])
     exchange_wait(cnts, cs, cr)
     total = jnp.sum(cnts[...], axis=0)
     recip = 1.0 / jnp.maximum(total, 1.0)
@@ -172,16 +182,18 @@
         inv[t] = jnp.broadcast_to(recip[:, t:t + 1], (1, DIM))
     for t in range(TASKS):
         grads(0, t, True)
-    to_2[1].wait_recv()
-    start(to_3[1])
+    to_2[0].wait_recv()
+    start(to_3[0])
     for cp in to_1:
         cp.wait_recv()
     acts(1)
+    to_2[1].wait_recv()
+    start(to_3[1])
     e_1.wait_recv()
+    for t in range(TASKS):
+        grads(1, t, False)
     to_2[2].wait_recv()
     start(to_3[2])
-    for t in range(TASKS):
-        grads(1, t, False)
     to_2[3].wait_recv()
     start(to_3[3])
     e_2.wait_recv()
@@ -244,48 +256,52 @@
     for dk, to in ((fx, to_x), (fz, to_za), (fx + fz, to_x + to_za - me)):
         back.append(start(rcopy(sb.at[own + dk], rb.at[own], to)))
     rb[own] = sb[own]
+    for t in range(TASKS):
+        for k in range(3):
+            o2_ref[t, pl.ds(k, 48, stride=3), :] = g2s[t, :, 128 * k:128 * (k + 1)]
+    for cp in back:
+        cp.wait_recv()
+    for t in range(TASKS):
+        parts = []
+        for b in range(32):
+            bza, bzb, by, bx, bc = b >> 4, (b >> 3) & 1, (b >> 2) & 1, (b >> 1) & 1, b & 1
+            at = 192 * bc + 96 * bzb + 48 * by
+            parts.append(rb[2 * bza + bx, t, :, at:at + 48])
+        full = jnp.concatenate(parts, axis=1)
+        for k in range(12):
+            o1_ref[t, pl.ds(k, 12, stride=12), :] = full[:12, 128 * k:128 * (k + 1)]
     exchange_wait(grams, gs, gr)
     m = jnp.sum(grams[...], axis=0)
-    ent = [m[:, i:i + 1] for i in range(6)]
+    ent = [jnp.broadcast_to(m[:, i:i + 1], (8, 128)) for i in range(6)]
+    neg = -TASKS / (ent[0] + ent[3] + ent[5])
     gram = {}
     for i, (t, s) in enumerate(pairs):
-        gram[t, s] = gram[s, t] = ent[i]
-    scale = (ent[0] + ent[3] + ent[5]) / TASKS
-
-    def solve(_, w):
-        up = []
-        for t in range(TASKS):
-            pull = gram[t, 0] * w[0] + gram[t, 1] * w[1] + gram[t, 2] * w[2]
-            up.append(w[t] * jnp.exp(-pull / scale))
-        tot = up[0] + up[1] + up[2]
-        return tuple(u / tot for u in up)
-    first = jnp.full((1, 1), 1.0 / TASKS, F32)
-    w = lax.fori_loop(0, SOLVER_STEPS, solve, (first, first, first))
-    al_ref[...] = jnp.concatenate(w, axis=1)
-    gg = w[0] * g2s[0] + w[1] * g2s[1] + w[2] * g2s[2]
-    for k in range(3):
-        o2_ref[pl.ds(k, 48, stride=3), :] = gg[:, 128 * k:128 * (k + 1)]
-    for cp in back:
-        cp.wait_recv()
-    for k in range(4):
-        o1_ref[k] = w[0] * rb[k, 0] + w[1] * rb[k, 1] + w[2] * rb[k, 2]
+        gram[t, s] = gram[s, t] = ent[i] * neg
+    w = [jnp.full((8, 128), 1.0 / TASKS, F32)] * TASKS
+    for _ in range(SOLVER_STEPS):
+        up = [w[t] * jnp.exp(gram[t, 0] * w[0] + gram[t, 1] * w[1] + gram[t, 2] * w[2]) for t in range(TASKS)]
+        norm = 1.0 / (up[0] + up[1] + up[2])
+        w = [u * norm for u in up]
+    al_ref[...] = jnp.where(lane == 0, w[0][:1], jnp.where(lane == 1, w[1][:1], w[2][:1]))[:, :TASKS]
     for cp in pending:
         cp.wait_send()
 
 
 def solution(mesh):
     def step(tokens, w_in, w_out, heads, lab, msk):
-        hp = jnp.pad(heads.transpose(0, 2, 1), ((0, 0), (0, PAD - CLS), (0, 0))).reshape(TASKS * PAD, DIM)
         vm = pl.BlockSpec(memory_space=pltpu.VMEM)
         dma = pltpu.SemaphoreType.DMA
-        alpha, o1, o2 = pl.pallas_call(
+        alpha, g1, g2 = pl.pallas_call(
             kernel,
             name="step",
-            out_shape=(jax.ShapeDtypeStruct((1, TASKS), F32), jax.ShapeDtypeStruct((4, 16, DIM), F32),
-                       jax.ShapeDtypeStruct((144, 128), F32)),
-            in_specs=[vm] * 6,
+            out_shape=(jax.ShapeDtypeStruct((1, TASKS), F32), jax.ShapeDtypeStruct((TASKS, 144, 128), F32),
+                       jax.ShapeDtypeStruct((TASKS, 144, 128), F32)),
+            in_specs=[pl.BlockSpec(memory_space=pl.ANY)] * 6,
             out_specs=(vm, vm, vm),
             scratch_shapes=[
+                pltpu.VMEM((TOK, DIM), BF16), pltpu.VMEM((DIM, HID), BF16), pltpu.VMEM((HID, DIM), BF16),
+                pltpu.VMEM((TASKS, CLS, DIM), BF16), pltpu.VMEM((TASKS, TOK), jnp.int32),
+                pltpu.VMEM((TASKS, TOK), jnp.int32), pltpu.VMEM((TASKS * PAD, DIM), BF16),
                 pltpu.VMEM((N_DEV, 1, 128), F32), pltpu.VMEM((N_DEV, 1, 128), F32),
                 pltpu.VMEM((4, DIM, TOK), BF16), pltpu.VMEM((4, TASKS, PAD, TOK), BF16),
                 pltpu.VMEM((TASKS, DIM, PAD), BF16), pltpu.VMEM((DIM, DIM), BF16), pltpu.VMEM((DIM, DIM), BF16),
@@ -298,11 +314,13 @@
                 pltpu.VMEM((TASKS, 48, DIM), F32), pltpu.VMEM((TASKS, 48, DIM), F32),
                 pltpu.VMEM((4, TASKS, 16, DIM), F32), pltpu.VMEM((4, TASKS, 16, DIM), F32),
                 dma((N_SEM,)), dma((N_SEM,)), dma((N_DEV,)), dma((N_DEV,)), dma((N_DEV,)), dma((N_DEV,)),
+                dma((6,)),
             ],
             compiler_params=pltpu.CompilerParams(collective_id=0, has_side_effects=True, vmem_limit_bytes=56 * 2**20),
-        )(tokens, w_in, w_out, hp, lab, msk)
-        g = o1[:, :12].reshape(2, 2, 12, 2, 2, 2, 48).transpose(2, 0, 4, 5, 1, 3, 6).reshape(-1)
-        return alpha.reshape(TASKS), g, o2.reshape(-1)
+        )(tokens, w_in, w_out, heads.transpose(0, 2, 1), lab, msk)
+        alpha = alpha.reshape(TASKS)
+        w = alpha[:, None, None]
+        return alpha, (w * g1).sum(axis=0).reshape(-1), (w * g2).sum(axis=0).reshape(-1)
 
     return jax.shard_map(step, mesh=mesh, in_specs=(P("data", None), P(), P(), P(), P(None, "data"), P(None, "data")),
                          out_specs=(P(), P("data"), P("data")), check_vma=False)

time: 83 us -> 69.7 us (0.84)
  Pallas kernels: 75.5 us -> 65.9 us
  local copies, waits for them, and re-layouts: 6.38 us -> 1.17 us
  other arithmetic: 0 us -> 1.81 us
    pallas_call x1, Pallas kernels: 75.5 us -> 65.9 us  [step(): pl.pallas_call(kernel, name='step', out_shape=(jax.ShapeDtypeStruct((1, T...]
    reduce_sum x0 -> x1, other arithmetic: none -> 1.81 us  [step(): (w * g2).sum(axis=0).reshape(-1)]
    unnamed x2 -> x1, local copies, waits for them, and re-layouts: 2.7 us -> 1.17 us
    pad x1 -> x0, local copies, waits for them, and re-layouts: 1.4 us -> none  [step(): jnp.pad(heads.transpose(0, 2, 1), ((0, 0), (0, PAD - CLS), (0, 0)))]
    reshape x2 -> x0, local copies, waits for them, and re-layouts: 1.26 us -> none  [step(): o1[:, :12].reshape(2, 2, 12, 2, 2, 2, 48).transpose(2, 0, 4, 5, 1, 3, 6)]
    slice x1 -> x0, local copies, waits for them, and re-layouts: 0.92 us -> none  [step(): o1[:, :12].reshape(2, 2, 12, 2, 2, 2, 48).transpose(2, 0, 4, 5, 1, 3, 6)]
where the time goes in v2:
time: 69.7 us; the launch traced here: 69.6 us
  Pallas kernels  65.9 us (95%)
  other arithmetic  1.81 us (3%)
  local copies, waits for them, and re-layouts  1.17 us (2%)
    pallas_call x1, Pallas kernels, step(): pl.pallas_call(kernel, name='step', out_shape=(jax.ShapeDtypeStruct((1, T...  65.9 us
    reduce_sum x1, other arithmetic, step(): (w * g2).sum(axis=0).reshape(-1)  1.81 us

profile of v2, /device:TPU:0, one launch (start us, length us, event | category | flops | bytes accessed | tf_op | source)
XLA Modules:
  0.0 69.6 jit_solution(195678698087533755)
XLA Ops:
  0.6 65.9 %step.1 = (f32[1,3]{1,0:T(1,128)}, f32[3,144,128]{2,1,0:T(8,128)}, f32[3,144,128]{2,1,0:T(8,128)}) custom-call(bf16[512,384]{1,0:T(8,128)(2,1)} %x_hbm.1, bf16[384,1536]{1,0:T(8,128)(2,1)} %w1_hbm.1, bf16[1536,384]{1,0:T(8,128)(2,1)} %w2_hbm.1, bf16[3,13,384]{2,1,0:T(8,128)(2,1)} %bitcast.6, s32[3,512]{1,0:T(4,128)} %lab_hbm.1, s32[3,512]{1,0:T(4,128)} %msk_hbm.1), custom_call_target="tpu_custom_call" | custom-call | tf_op jit(solution)/shard_map/step/pallas_call | solution.py:294
  66.6 1.8 %multiply_reduce_fusion = (f32[144,128]{1,0:T(8,128)}, f32[144,128]{1,0:T(8,128)}) fusion(f32[3,144,128]{2,1,0:T(8,128)} %get-tuple-element.8, f32[3]{0:T(128)} %bitcast.7, f32[3,144,128]{2,1,0:T(8,128)} %get-tuple-element.7), kind=kLoop, calls=%fused_computation | loop fusion | flops 184320 | bytes 589836 | tf_op jit(solution)/shard_map/reduce_sum | solution.py:323
  68.4 1.2 %copy.10 = f32[3]{0:T(128)} copy(f32[3]{0:T(128)} %bitcast.8) | data formatting | bytes 24

commit v3 on v2

v3 whole, which is shorter than its diff:
```python
import jax
import jax.numpy as jnp
from jax import lax
from jax.experimental import pallas as pl
from jax.experimental.pallas import tpu as pltpu
from jax.sharding import PartitionSpec as P

MESH = pl.DeviceIdType.MESH
SOLVER_STEPS = 20
N_DEV = 32
TOK, DIM, HID, TASKS, CLS, PAD = 512, 384, 1536, 3, 13, 16
HALF = TOK // 2
GELU_C = 0.7978845608028654
GELU_A = 0.044715
N_SEM = 69
OWN, FROM_X, FROM_Z, FROM_XZ, FROM_Y, FROM_YZ = range(6)

F32, BF16 = jnp.float32, jnp.bfloat16


def dot(a, b):
    return jnp.dot(a, b, preferred_element_type=F32)


def dot_nt(a, b):
    return lax.dot_general(a, b, (((1,), (1,)), ((), ())), preferred_element_type=F32)


def gelu_cdf(p):
    sq = p * p
    t = jnp.tanh(GELU_C * (p + GELU_A * (sq * p)))
    return sq, t, 0.5 * (1.0 + t)


def kernel(x_hbm, w1_hbm, w2_hbm, h_hbm, lab_hbm, msk_hbm, al_ref, o1_ref, o2_ref,
           x_ref, w1_ref, w2_ref, h_ref, lab_ref, msk_ref, hp_ref, cnts, grams,
           gx, ge, ht, w1a, w1b, w2a, a_own, at, gp, dz, dzx, qt, inv, acc1, acc2,
           rc1, rc2, ra1, ra2, rb1, rb2, g1s, g2s, sb, rb,
           ss, rs, ls):
    me = lax.axis_index("data")
    c = lax.rem(me, 2)
    x = lax.rem(me // 2, 2)
    y = lax.rem(me // 4, 2)
    zl = lax.rem(me // 8, 2)
    zh = lax.rem(me // 16, 2)
    to_c = me + (1 - 2 * c)
    to_x = me + 2 * (1 - 2 * x)
    to_y = me + 4 * (1 - 2 * y)
    to_zl = me + 8 * (1 - 2 * zl)
    to_zh = me + 16 * (1 - 2 * zh)

    used = []

    def rcopy(src, dst, dev, group):
        i = len(used)
        used.append(i)
        return pltpu.make_async_remote_copy(src_ref=src, dst_ref=dst, send_sem=ss.at[group], recv_sem=rs.at[i],
                                            device_id=(dev,), device_id_type=MESH)

    def start(cp):
        cp.start()
        return cp

    def wait_bytes(ref, sem):
        pltpu.make_async_copy(ref, ref, sem).wait()

    def row_copy(buf, src_row, send_sem, recv_sem, dev):
        return pltpu.make_async_remote_copy(src_ref=buf.at[src_row], dst_ref=buf.at[src_row], send_sem=send_sem,
                                            recv_sem=recv_sem, device_id=(dev,), device_id_type=MESH)

    def exchange_start(buf, s_sem, r_sem):
        def go(i, _):
            row_copy(buf, me, s_sem, r_sem, lax.rem(me + i, N_DEV)).start()
            return 0
        lax.fori_loop(1, N_DEV, go, 0)

    def exchange_wait(buf, sem):
        wait_bytes(buf.at[pl.ds(0, N_DEV - 1)], sem)

    loads = [pltpu.make_async_copy(a, b, ls.at[i]) for i, (a, b) in enumerate((
        (x_hbm, x_ref), (msk_hbm, msk_ref), (w1_hbm, w1_ref), (w2_hbm, w2_ref), (h_hbm, h_ref), (lab_hbm, lab_ref)))]
    for cp in loads:
        cp.start()

    bar = pltpu.get_barrier_semaphore()

    def sig(i, _):
        pl.semaphore_signal(bar, inc=1, device_id=(lax.rem(me + i, N_DEV),), device_id_type=MESH)
        return 0
    lax.fori_loop(1, N_DEV, sig, 0)

    col = lax.broadcasted_iota(jnp.int32, (DIM, 1), 0)
    blk = (col * 43691) >> 19
    dev = ((blk >> 3) & 1) + 4 * ((blk >> 2) & 1) + 8 * ((blk >> 1) & 1) + 16 * ((blk >> 4) & 1) + 2 * (blk & 1)
    perm = (lax.broadcasted_iota(jnp.int32, (DIM, DIM), 1) == 12 * dev + (col - 12 * blk)).astype(BF16)
    loads[0].wait()
    for h in range(2):
        gx[OWN, h] = dot_nt(perm, x_ref[HALF * h:HALF * (h + 1), :]).astype(BF16)
    lane = lax.broadcasted_iota(jnp.int32, (1, 128), 1)
    row = jnp.zeros((1, 128), F32)
    loads[1].wait()
    for t in range(TASKS):
        row = row + jnp.where(lane == t, jnp.sum(msk_ref[t:t + 1, :].astype(F32), axis=1, keepdims=True), 0.0)
    cnts[me] = row

    pl.semaphore_wait(bar, N_DEV - 1)

    def piece(slot, h, r0=0, n=DIM):
        return gx.at[slot, h, pl.ds(r0, n)]
    cuts = ((0, 0, 192), (0, 192, 192), (1, 0, 192), (1, 192, 128), (1, 320, 64))
    z_x = [rcopy(piece(OWN, *k), piece(FROM_Z, *k), to_zh, 0) for k in cuts]
    x_x = [rcopy(piece(OWN, h), piece(FROM_X, h), to_x, 0) for h in range(2)]
    y_x = [rcopy(piece(OWN, h), piece(FROM_Y, h), to_y, 0) for h in range(2)]
    xz_x = [rcopy(piece(FROM_Z, *k), piece(FROM_XZ, *k), to_x, 0) for k in cuts]
    yz_x = [rcopy(piece(FROM_Z, *k), piece(FROM_YZ, *k), to_y, 0) for k in cuts]
    z_e = rcopy(ge.at[OWN], ge.at[FROM_Z], to_zh, 1)
    x_e = rcopy(ge.at[OWN], ge.at[FROM_X], to_x, 1)
    y_e = rcopy(ge.at[OWN], ge.at[FROM_Y], to_y, 1)
    xz_e = rcopy(ge.at[FROM_Z], ge.at[FROM_XZ], to_x, 1)
    yz_e = rcopy(ge.at[FROM_Z], ge.at[FROM_YZ], to_y, 1)

    def forward(got, a, b):
        got.wait_recv()
        start(a)
        start(b)

    exchange_start(cnts, ls.at[6], ls.at[7])
    start(z_x[0])
    start(x_x[0])
    start(y_x[0])

    for cp in loads[2:]:
        cp.wait()
    hp_ref[...] = jnp.zeros_like(hp_ref)
    for t in range(TASKS):
        hp_ref[PAD * t:PAD * t + CLS, :] = h_ref[t]

    def fwd(i, _):
        cols = pl.ds(pl.multiple_of(i * 256, 256), 256)
        p = dot(x_ref[...], w1_ref[:, cols])
        a_own[:, cols] = (p * gelu_cdf(p)[2]).astype(BF16)
        return 0
    lax.fori_loop(0, HID // 256, fwd, 0)
    start(z_x[1])
    z = (x_ref[...].astype(F32) + dot(a_own[...], w2_ref[...])).astype(BF16)
    logits = dot_nt(hp_ref[...], z)
    cls = lax.broadcasted_iota(jnp.int32, (PAD, TOK), 0)
    valid = cls < CLS
    for t in range(TASKS):
        lg = jnp.where(valid, logits[PAD * t:PAD * (t + 1)], -jnp.inf)
        ex = jnp.exp(lg - jnp.max(lg, axis=0, keepdims=True))
        sm = ex / jnp.sum(ex, axis=0, keepdims=True)
        hot = (lab_ref[t:t + 1, :] == cls).astype(F32)
        ge[OWN, t] = jnp.where(valid, msk_ref[t:t + 1, :].astype(F32) * (sm - hot), 0.0).astype(BF16)
    start(z_e)
    start(x_e)
    start(y_e)
    start(x_x[1])
    start(y_x[1])

    hid_iota = lax.broadcasted_iota(jnp.int32, (DIM, HID), 1)
    seg = (col * 43691) >> 21
    src_a = 48 * ((seg >> 2) + 8 * ((seg >> 1) & 1) + 4 * (seg & 1) + 16 * zh + 2 * x) + (col - 48 * seg)
    seg = (col * 43691) >> 20
    src_b = (48 * (((seg >> 2) & 1) + 2 * ((seg >> 1) & 1) + 8 * (seg & 1) + 16 * zh + 4 * y)
             + 24 * (seg >> 3) + (col - 24 * seg))
    for src, dst in ((src_a, w1a), (src_b, w1b)):
        sel = (hid_iota == src).astype(BF16)
        dst[...] = dot_nt(dot_nt(sel, w1_ref[...]).astype(BF16), perm).astype(BF16)
    for k in range(8):
        dv = (k >> 2) + 8 * ((k >> 1) & 1) + 4 * (k & 1) + 16 * zh + 2 * x
        w2a[48 * k:48 * (k + 1), :] = w2_ref[pl.ds(pl.multiple_of(48 * dv, 16), 48), :]
    for t in range(TASKS):
        ht[t] = jnp.transpose(hp_ref[PAD * t:PAD * (t + 1), :].astype(F32)).astype(BF16)

    strips = [slice(128 * r, 128 * (r + 1)) for r in range(3)]

    def slope(s, h):
        for rows in strips:
            p = dot(w1a[rows, :], gx[s, h])
            sq, t, cdf = gelu_cdf(p)
            gp[rows, :] = cdf + (0.5 * GELU_C) * p * (1.0 - t * t) * (1.0 + (3.0 * GELU_A) * sq)

    def act(s, h, k):
        for rows in strips:
            p = dot(w1b[rows, :], gx[s, h])
            at[k, h, rows, :] = (p * gelu_cdf(p)[2]).astype(BF16)

    def dz_of(s, h, t, ref):
        ref[...] = dot(ht[t], ge[s, t, :, HALF * h:HALF * (h + 1)]).astype(BF16)

    def q_of(h, t, k, ref):
        for rows in strips:
            qt[k, t, h, rows, :] = (dot(w2a[rows, :], ref[...]) * gp[rows, :]).astype(BF16)

    def prep_a(s, h, k):
        slope(s, h)
        for t in range(TASKS):
            dz_of(s, h, t, dzx)
            q_of(h, t, k, dzx)

    def prep_b(s, h, k):
        act(s, h, k)
        for t in range(TASKS):
            dz_of(s, h, t, dz.at[k, t, h])

    def prep(s, h):
        slope(s, h)
        act(s, h, 0)
        for t in range(TASKS):
            dz_of(s, h, t, dz.at[0, t, h])
            q_of(h, t, 0, dz.at[0, t, h])

    def add_a(s, t, k, first=False):
        d = dot_nt(gx[s, 0], qt[k, t, 0]) + dot_nt(gx[s, 1], qt[k, t, 1])
        d = (d * inv[t]).astype(BF16).astype(F32)
        acc1[t] = d if first else acc1[t] + d

    def add_b(t, k, first=False):
        d = dot_nt(at[k, 0], dz[k, t, 0]) + dot_nt(at[k, 1], dz[k, t, 1])
        d = (d * inv[t]).astype(BF16).astype(F32)
        acc2[t] = d if first else acc2[t] + d

    prep(OWN, 0)
    prep(OWN, 1)
    start(z_x[2])
    exchange_wait(cnts, ls.at[7])
    total = jnp.sum(cnts[...], axis=0)
    recip = 1.0 / jnp.maximum(total, 1.0)
    for t in range(TASKS):
        inv[t] = jnp.broadcast_to(recip[:, t:t + 1], (1, DIM))
    for t in range(TASKS):
        add_a(OWN, t, 0, True)
        add_b(t, 0, True)
    start(z_x[3])
    for cp in (x_e, x_x[0], x_x[1]):
        cp.wait_recv()
    prep_a(FROM_X, 0, 0)
    start(z_x[4])
    forward(z_x[0], xz_x[0], yz_x[0])
    prep_a(FROM_X, 1, 0)
    for t in range(TASKS):
        add_a(FROM_X, t, 0)
    for cp in (y_e, y_x[0], y_x[1]):
        cp.wait_recv()
    prep_b(FROM_Y, 0, 0)
    prep_b(FROM_Y, 1, 0)
    for t in range(TASKS):
        add_b(t, 0)
    forward(z_e, xz_e, yz_e)
    forward(z_x[1], xz_x[1], yz_x[1])
    prep(FROM_Z, 0)
    forward(z_x[2], xz_x[2], yz_x[2])
    forward(z_x[3], xz_x[3], yz_x[3])
    forward(z_x[4], xz_x[4], yz_x[4])
    for cp in (xz_e, xz_x[0], xz_x[1]):
        cp.wait_recv()
    prep_a(FROM_XZ, 0, 1)
    for cp in (yz_e, yz_x[0], yz_x[1]):
        cp.wait_recv()
    prep_b(FROM_YZ, 0, 1)
    prep(FROM_Z, 1)
    for cp in xz_x[2:]:
        cp.wait_recv()
    for cp in yz_x[2:]:
        cp.wait_recv()

    def rows(base, n):
        return pl.ds(pl.multiple_of(base, 8), n)
    bits1, bits2 = (c, y, zl), (c, x, zl)
    dest1, dest2 = (to_c, to_y, to_zl), (to_c, to_x, to_zl)
    size = (96, 48, 24)

    def base(bits, u, stage):
        at0 = 192 * u
        for i in range(stage):
            at0 = at0 + size[i] * bits[i]
        return at0

    def send(acc, recv, bits, dest, t, u, stage, group):
        at0 = base(bits, u, stage) + size[stage] * (1 - bits[stage])
        return start(rcopy(acc.at[t, rows(at0, size[stage])], recv.at[t, u], dest[stage], group))

    part1 = (acc1, (rc1, ra1, rb1), bits1, dest1)
    part2 = (acc2, (rc2, ra2, rb2), bits2, dest2)
    order = [(t, u) for t in range(TASKS) for u in range(2)]
    cps = {}

    def go(part, i, t, u, stage):
        acc, recv, bits, dest = part
        cps[i, t, u, stage] = send(acc, recv[stage], bits, dest, t, u, stage, 2 * stage + i + 1)

    def merge(part, t, u, stage):
        acc, recv, bits, _ = part
        mine = rows(base(bits, u, stage) + size[stage] * bits[stage], size[stage])
        v = acc[t, mine] + recv[stage][t, u]
        acc[t, mine] = v
        return v

    def add(part, i, t, u, stage):
        cps[i, t, u, stage].wait_recv()
        return merge(part, t, u, stage)

    own = 2 * zh + x
    fx, fz = 1 - 2 * x, 2 * (1 - 2 * zh)
    back = []

    def send_back(t):
        for dk, to in ((fz, to_zh), (fx + fz, to_x + to_zh - me), (fx, to_x)):
            back.append(start(rcopy(sb.at[own + dk, t], rb.at[own, t], to, 8)))

    def finish(t, u):
        g = add(part1, 1, t, u, 2)
        g1s[t, 24 * u:24 * (u + 1)] = g
        for k in range(2):
            sb[2 * u + k, t] = g[12 * k:12 * (k + 1)]
        if u == 1 and t < TASKS - 1:
            send_back(t)
        g2s[t, 24 * u:24 * (u + 1)] = add(part2, 2, t, u, 2)

    both = ((1, part1), (2, part2))

    def first_hop(n):
        for i, part in both:
            add(part, i, *order[n], 0)
            go(part, i, *order[n], 1)

    slope(FROM_XZ, 1)
    act(FROM_YZ, 1, 1)
    for t in range(TASKS):
        dz_of(FROM_XZ, 1, t, dzx)
        q_of(1, t, 1, dzx)
        add_a(FROM_Z, t, 0)
        add_a(FROM_XZ, t, 1)
        for u in range(2):
            go(part1, 1, t, u, 0)
        dz_of(FROM_YZ, 1, t, dz.at[1, t, 1])
        add_b(t, 0)
        add_b(t, 1)
        for u in range(2):
            go(part2, 2, t, u, 0)
        if t == 1:
            first_hop(0)
            first_hop(1)
    first_hop(2)
    for n in range(6):
        if n + 3 < 6:
            for i, part in both:
                add(part, i, *order[n + 3], 0)
        for i, part in both:
            cps[i, *order[n], 1].wait_recv()
            if n + 3 < 6:
                go(part, i, *order[n + 3], 1)
            merge(part, *order[n], 1)
            go(part, i, *order[n], 2)
        if n >= 2:
            finish(*order[n - 2])
    finish(*order[4])
    finish(*order[5])

    row = jnp.zeros((1, 128), F32)
    pairs = [(0, 0), (0, 1), (0, 2), (1, 1), (1, 2), (2, 2)]
    for i, (t, s) in enumerate(pairs):
        part = jnp.sum(g1s[t] * g1s[s] + g2s[t] * g2s[s], axis=0, keepdims=True)
        row = row + jnp.where(lane == i, jnp.sum(part, axis=1, keepdims=True), 0.0)
    grams[me] = row
    exchange_start(grams, ls.at[8], ls.at[9])
    send_back(TASKS - 1)
    rb[own] = sb[own]
    for t in range(TASKS):
        for k in range(3):
            o2_ref[t, pl.ds(k, 48, stride=3), :] = g2s[t, :, 128 * k:128 * (k + 1)]
    for cp in back:
        cp.wait_recv()
    for t in range(TASKS):
        parts = []
        for b in range(32):
            bzh, bzl, by, bx, bc = b >> 4, (b >> 3) & 1, (b >> 2) & 1, (b >> 1) & 1, b & 1
            at0 = 192 * bc + 96 * bzl + 48 * by
            parts.append(rb[2 * bzh + bx, t, :, at0:at0 + 48])
        full = jnp.concatenate(parts, axis=1)
        for k in range(12):
            o1_ref[t, pl.ds(k, 12, stride=12), :] = full[:, 128 * k:128 * (k + 1)]
    exchange_wait(grams, ls.at[9])
    m = jnp.sum(grams[...], axis=0)
    ent = [jnp.broadcast_to(m[:, i:i + 1], (8, 128)) for i in range(6)]
    neg = -TASKS / (ent[0] + ent[3] + ent[5])
    gram = {}
    for i, (t, s) in enumerate(pairs):
        gram[t, s] = gram[s, t] = ent[i] * neg
    w = [jnp.full((8, 128), 1.0 / TASKS, F32)] * TASKS
    for _ in range(SOLVER_STEPS):
        up = [w[t] * jnp.exp(gram[t, 0] * w[0] + gram[t, 1] * w[1] + gram[t, 2] * w[2]) for t in range(TASKS)]
        norm = 1.0 / (up[0] + up[1] + up[2])
        w = [v * norm for v in up]
    al_ref[...] = jnp.where(lane == 0, w[0][:1], jnp.where(lane == 1, w[1][:1], w[2][:1]))[:, :TASKS]
    exchange_wait(cnts, ls.at[6])
    exchange_wait(grams, ls.at[8])
    for i, ref in enumerate((gx.at[pl.ds(0, 5)], ge.at[pl.ds(0, 5)], rc1, rc2, ra1, ra2, rb1, rb2, rb.at[pl.ds(0, 3)])):
        wait_bytes(ref, ss.at[i])


def solution(mesh):
    def step(tokens, w_in, w_out, heads, lab, msk):
        vm = pl.BlockSpec(memory_space=pltpu.VMEM)
        dma = pltpu.SemaphoreType.DMA
        v = pltpu.VMEM
        alpha, g1, g2 = pl.pallas_call(
            kernel,
            name="step",
            out_shape=(jax.ShapeDtypeStruct((1, TASKS), F32), jax.ShapeDtypeStruct((TASKS, 144, 128), F32),
                       jax.ShapeDtypeStruct((TASKS, 144, 128), F32)),
            in_specs=[pl.BlockSpec(memory_space=pltpu.HBM)] * 6,
            out_specs=(vm, vm, vm),
            scratch_shapes=[
                v((TOK, DIM), BF16), v((DIM, HID), BF16), v((HID, DIM), BF16),
                v((TASKS, CLS, DIM), BF16), v((TASKS, TOK), jnp.int32),
                v((TASKS, TOK), jnp.int32), v((TASKS * PAD, DIM), BF16),
                v((N_DEV, 1, 128), F32), v((N_DEV, 1, 128), F32),
                v((6, 2, DIM, HALF), BF16), v((6, TASKS, PAD, TOK), BF16),
                v((TASKS, DIM, PAD), BF16), v((DIM, DIM), BF16), v((DIM, DIM), BF16), v((DIM, DIM), BF16),
                v((TOK, HID), BF16), v((2, 2, DIM, HALF), BF16), v((DIM, HALF), F32),
                v((2, TASKS, 2, DIM, HALF), BF16), v((DIM, HALF), BF16), v((2, TASKS, 2, DIM, HALF), BF16),
                v((TASKS, 1, DIM), F32),
                v((TASKS, DIM, DIM), F32), v((TASKS, DIM, DIM), F32),
                v((TASKS, 2, 96, DIM), F32), v((TASKS, 2, 96, DIM), F32),
                v((TASKS, 2, 48, DIM), F32), v((TASKS, 2, 48, DIM), F32),
                v((TASKS, 2, 24, DIM), F32), v((TASKS, 2, 24, DIM), F32),
                v((TASKS, 48, DIM), F32), v((TASKS, 48, DIM), F32),
                v((4, TASKS, 12, DIM), F32), v((4, TASKS, 12, DIM), F32),
                dma((9,)), dma((N_SEM,)), dma((10,)),
            ],
            compiler_params=pltpu.CompilerParams(collective_id=0, has_side_effects=True, vmem_limit_bytes=28 * 2**20),
        )(*[pltpu.with_memory_space_constraint(a, pltpu.HBM)
            for a in (tokens, w_in, w_out, heads.transpose(0, 2, 1), lab, msk)])
        alpha = alpha.reshape(TASKS)
        w = alpha[:, None, None]
        return alpha, (w * g1).sum(axis=0).reshape(-1), (w * g2).sum(axis=0).reshape(-1)

    return jax.shard_map(step, mesh=mesh, in_specs=(P("data", None), P(), P(), P(), P(None, "data"), P(None, "data")),
                         out_specs=(P(), P("data"), P("data")), check_vma=False)
```

time: 69.7 us -> 60.9 us (0.87)
  Pallas kernels: 65.9 us -> 58.9 us
  other arithmetic: 1.81 us -> 0.74 us
    pallas_call x1, Pallas kernels: 65.9 us -> 58.9 us  [step(): pl.pallas_call(kernel, name='step', out_shape=(jax.ShapeDtypeStruct((1, T...]
    reduce_sum x1, other arithmetic: 1.81 us -> 0.74 us  [step(): (w * g2).sum(axis=0).reshape(-1)]
where the time goes in v3:
time: 60.9 us; the launch traced here: 60.8 us
  Pallas kernels  58.9 us (97%)
  other arithmetic  0.74 us (1%)
  between operations  0.64 us (1%)
    pallas_call x1, Pallas kernels, step(): pl.pallas_call(kernel, name='step', out_shape=(jax.ShapeDtypeStruct((1, T...  58.9 us

profile of v3, /device:TPU:0, one launch (start us, length us, event | category | flops | bytes accessed | tf_op | source)
XLA Modules:
  0.0 60.8 jit_solution(17425524400431463610)
XLA Ops:
  0.6 58.9 %step.1 = (f32[1,3]{1,0:T(1,128)S(1)}, f32[3,144,128]{2,1,0:T(8,128)S(1)}, f32[3,144,128]{2,1,0:T(8,128)S(1)}) custom-call(bf16[512,384]{1,0:T(8,128)(2,1)} %x_hbm.1, bf16[384,1536]{1,0:T(8,128)(2,1)} %w1_hbm.1, bf16[1536,384]{1,0:T(8,128)(2,1)} %w2_hbm.1, bf16[3,13,384]{2,1,0:T(8,128)(2,1)} %bitcast.8, s32[3,512]{1,0:T(4,128)} %lab_hbm.1, s32[3,512]{1,0:T(4,128)} %msk_hbm.1), custom_call_target="tpu_custom_call" | custom-call | tf_op jit(solution)/shard_map/step/pallas_call | solution.py:408
  59.5 0.7 %multiply_reduce_fusion = (f32[144,128]{1,0:T(8,128)}, f32[144,128]{1,0:T(8,128)}) fusion(f32[3,144,128]{2,1,0:T(8,128)S(1)} %get-tuple-element.8, f32[3]{0:T(128)S(1)} %bitcast.4, f32[3,144,128]{2,1,0:T(8,128)S(1)} %get-tuple-element.7), kind=kLoop, calls=%fused_computation | loop fusion | flops 184320 | bytes 589836 | tf_op jit(solution)/shard_map/reduce_sum | solution.py:438
  60.2 0.5 copy.10

commit v4 on v3

--- a/solution.py
+++ b/solution.py
@@ -12,7 +12,7 @@
 HALF = TOK // 2
 GELU_C = 0.7978845608028654
 GELU_A = 0.044715
-N_SEM = 69
+N_SEM = 68
 OWN, FROM_X, FROM_Z, FROM_XZ, FROM_Y, FROM_YZ = range(6)
 
 F32, BF16 = jnp.float32, jnp.bfloat16
@@ -47,7 +47,8 @@
     to_x = me + 2 * (1 - 2 * x)
     to_y = me + 4 * (1 - 2 * y)
     to_zl = me + 8 * (1 - 2 * zl)
-    to_zh = me + 16 * (1 - 2 * zh)
+    to_zh = me + 16 * (1 - 2 * zh) + 8 * (1 - 2 * zl)
+    e = lax.rem(zh + zl, 2)
 
     used = []
 
@@ -91,7 +92,8 @@
 
     col = lax.broadcasted_iota(jnp.int32, (DIM, 1), 0)
     blk = (col * 43691) >> 19
-    dev = ((blk >> 3) & 1) + 4 * ((blk >> 2) & 1) + 8 * ((blk >> 1) & 1) + 16 * ((blk >> 4) & 1) + 2 * (blk & 1)
+    dev = (((blk >> 3) & 1) + 4 * ((blk >> 2) & 1) + 8 * (((blk >> 1) ^ (blk >> 4)) & 1) + 16 * ((blk >> 4) & 1)
+           + 2 * (blk & 1))
     perm = (lax.broadcasted_iota(jnp.int32, (DIM, DIM), 1) == 12 * dev + (col - 12 * blk)).astype(BF16)
     loads[0].wait()
     for h in range(2):
@@ -119,6 +121,13 @@
     xz_e = rcopy(ge.at[FROM_Z], ge.at[FROM_XZ], to_x, 1)
     yz_e = rcopy(ge.at[FROM_Z], ge.at[FROM_YZ], to_y, 1)
 
+    outer, inner = e == 0, e == 1
+
+    def start_if(cond, cp):
+        @pl.when(cond)
+        def _():
+            cp.start()
+
     def forward(got, a, b):
         got.wait_recv()
         start(a)
@@ -141,7 +150,7 @@
         a_own[:, cols] = (p * gelu_cdf(p)[2]).astype(BF16)
         return 0
     lax.fori_loop(0, HID // 256, fwd, 0)
-    start(z_x[1])
+    start_if(inner, z_x[1])
     z = (x_ref[...].astype(F32) + dot(a_own[...], w2_ref[...])).astype(BF16)
     logits = dot_nt(hp_ref[...], z)
     cls = lax.broadcasted_iota(jnp.int32, (PAD, TOK), 0)
@@ -152,7 +161,8 @@
         sm = ex / jnp.sum(ex, axis=0, keepdims=True)
         hot = (lab_ref[t:t + 1, :] == cls).astype(F32)
         ge[OWN, t] = jnp.where(valid, msk_ref[t:t + 1, :].astype(F32) * (sm - hot), 0.0).astype(BF16)
-    start(z_e)
+    start_if(inner, z_e)
+    start_if(outer, z_x[1])
     start(x_e)
     start(y_e)
     start(x_x[1])
@@ -160,15 +170,16 @@
 
     hid_iota = lax.broadcasted_iota(jnp.int32, (DIM, HID), 1)
     seg = (col * 43691) >> 21
-    src_a = 48 * ((seg >> 2) + 8 * ((seg >> 1) & 1) + 4 * (seg & 1) + 16 * zh + 2 * x) + (col - 48 * seg)
+    src_a = 48 * ((seg >> 2) + 8 * (((seg >> 1) & 1) ^ zh) + 4 * (seg & 1) + 16 * zh + 2 * x) + (col - 48 * seg)
     seg = (col * 43691) >> 20
-    src_b = (48 * (((seg >> 2) & 1) + 2 * ((seg >> 1) & 1) + 8 * (seg & 1) + 16 * zh + 4 * y)
+    src_b = (48 * (((seg >> 2) & 1) + 2 * ((seg >> 1) & 1) + 8 * ((seg & 1) ^ zh) + 16 * zh + 4 * y)
              + 24 * (seg >> 3) + (col - 24 * seg))
     for src, dst in ((src_a, w1a), (src_b, w1b)):
         sel = (hid_iota == src).astype(BF16)
         dst[...] = dot_nt(dot_nt(sel, w1_ref[...]).astype(BF16), perm).astype(BF16)
     for k in range(8):
-        dv = (k >> 2) + 8 * ((k >> 1) & 1) + 4 * (k & 1) + 16 * zh + 2 * x
+        eb = (k >> 1) & 1
+        dv = (k >> 2) + 8 * (eb + zh - 2 * eb * zh) + 4 * (k & 1) + 16 * zh + 2 * x
         w2a[48 * k:48 * (k + 1), :] = w2_ref[pl.ds(pl.multiple_of(48 * dv, 16), 48), :]
     for t in range(TASKS):
         ht[t] = jnp.transpose(hp_ref[PAD * t:PAD * (t + 1), :].astype(F32)).astype(BF16)
@@ -221,9 +232,11 @@
         d = (d * inv[t]).astype(BF16).astype(F32)
         acc2[t] = d if first else acc2[t] + d
 
+    start_if(outer, z_e)
+    start_if(inner, z_x[2])
     prep(OWN, 0)
     prep(OWN, 1)
-    start(z_x[2])
+    start_if(inner, z_x[3])
     exchange_wait(cnts, ls.at[7])
     total = jnp.sum(cnts[...], axis=0)
     recip = 1.0 / jnp.maximum(total, 1.0)
@@ -232,54 +245,59 @@
     for t in range(TASKS):
         add_a(OWN, t, 0, True)
         add_b(t, 0, True)
-    start(z_x[3])
+    start_if(inner, z_x[4])
+    start_if(outer, z_x[2])
     for cp in (x_e, x_x[0], x_x[1]):
         cp.wait_recv()
+    forward(z_x[0], xz_x[0], yz_x[0])
     prep_a(FROM_X, 0, 0)
-    start(z_x[4])
-    forward(z_x[0], xz_x[0], yz_x[0])
+    start_if(outer, z_x[3])
+    forward(z_e, xz_e, yz_e)
+    forward(z_x[1], xz_x[1], yz_x[1])
     prep_a(FROM_X, 1, 0)
     for t in range(TASKS):
         add_a(FROM_X, t, 0)
+    start_if(outer, z_x[4])
     for cp in (y_e, y_x[0], y_x[1]):
         cp.wait_recv()
     prep_b(FROM_Y, 0, 0)
     prep_b(FROM_Y, 1, 0)
     for t in range(TASKS):
         add_b(t, 0)
-    forward(z_e, xz_e, yz_e)
-    forward(z_x[1], xz_x[1], yz_x[1])
+    forward(z_x[2], xz_x[2], yz_x[2])
     prep(FROM_Z, 0)
-    forward(z_x[2], xz_x[2], yz_x[2])
     forward(z_x[3], xz_x[3], yz_x[3])
     forward(z_x[4], xz_x[4], yz_x[4])
+    prep(FROM_Z, 1)
     for cp in (xz_e, xz_x[0], xz_x[1]):
         cp.wait_recv()
     prep_a(FROM_XZ, 0, 1)
     for cp in (yz_e, yz_x[0], yz_x[1]):
         cp.wait_recv()
     prep_b(FROM_YZ, 0, 1)
-    prep(FROM_Z, 1)
+    add_a(FROM_Z, 0, 0)
     for cp in xz_x[2:]:
-        cp.wait_recv()
-    for cp in yz_x[2:]:
         cp.wait_recv()
 
     def rows(base, n):
         return pl.ds(pl.multiple_of(base, 8), n)
-    bits1, bits2 = (c, y, zl), (c, x, zl)
+    bits1, bits2 = (c, y, e), (c, x, e)
     dest1, dest2 = (to_c, to_y, to_zl), (to_c, to_x, to_zl)
-    size = (96, 48, 24)
-
-    def base(bits, u, stage):
+    z_first = ((0, 0),)
+
+    def moves(bits, t, u, stage):
         at0 = 192 * u
-        for i in range(stage):
-            at0 = at0 + size[i] * bits[i]
-        return at0
-
-    def send(acc, recv, bits, dest, t, u, stage, group):
-        at0 = base(bits, u, stage) + size[stage] * (1 - bits[stage])
-        return start(rcopy(acc.at[t, rows(at0, size[stage])], recv.at[t, u], dest[stage], group))
+        if stage == 0:
+            return [(at0 + 96 * (1 - bits[0]), at0 + 96 * bits[0], 0, 96, 0)]
+        at0 = at0 + 96 * bits[0]
+        if (t, u) in z_first:
+            if stage == 1:
+                return [(at0 + 48 * b + 24 * (1 - bits[2]), at0 + 48 * b + 24 * bits[2], 24 * b, 24, 2) for b in range(2)]
+            return [(at0 + 48 * (1 - bits[1]) + 24 * bits[2], at0 + 48 * bits[1] + 24 * bits[2], 0, 24, 1)]
+        if stage == 1:
+            return [(at0 + 48 * (1 - bits[1]), at0 + 48 * bits[1], 0, 48, 1)]
+        at0 = at0 + 48 * bits[1]
+        return [(at0 + 24 * (1 - bits[2]), at0 + 24 * bits[2], 0, 24, 2)]
 
     part1 = (acc1, (rc1, ra1, rb1), bits1, dest1)
     part2 = (acc2, (rc2, ra2, rb2), bits2, dest2)
@@ -288,34 +306,45 @@
 
     def go(part, i, t, u, stage):
         acc, recv, bits, dest = part
-        cps[i, t, u, stage] = send(acc, recv[stage], bits, dest, t, u, stage, 2 * stage + i + 1)
+        cps[i, t, u, stage] = [
+            start(rcopy(acc.at[t, rows(out, n)], recv[stage].at[t, u, pl.ds(at0, n)], dest[link], 2 * stage + i + 1))
+            for out, _, at0, n, link in moves(bits, t, u, stage)]
 
     def merge(part, t, u, stage):
         acc, recv, bits, _ = part
-        mine = rows(base(bits, u, stage) + size[stage] * bits[stage], size[stage])
-        v = acc[t, mine] + recv[stage][t, u]
-        acc[t, mine] = v
+        for _, kept, at0, n, _ in moves(bits, t, u, stage):
+            mine = rows(kept, n)
+            v = acc[t, mine] + recv[stage][t, u, at0:at0 + n]
+            acc[t, mine] = v
         return v
 
+    def arrived(i, t, u, stage):
+        for cp in cps[i, t, u, stage]:
+            cp.wait_recv()
+
     def add(part, i, t, u, stage):
-        cps[i, t, u, stage].wait_recv()
+        arrived(i, t, u, stage)
         return merge(part, t, u, stage)
 
     own = 2 * zh + x
     fx, fz = 1 - 2 * x, 2 * (1 - 2 * zh)
     back = []
 
-    def send_back(t):
+    for part in (pl.ds(0, 24), pl.ds(24, 16)):
         for dk, to in ((fz, to_zh), (fx + fz, to_x + to_zh - me), (fx, to_x)):
-            back.append(start(rcopy(sb.at[own + dk, t], rb.at[own, t], to, 8)))
+            back.append(rcopy(sb.at[own + dk, part], rb.at[own, part], to, 8))
+
+    def send_back(which, cond):
+        @pl.when(cond)
+        def _():
+            for cp in back[3 * which:3 * which + 3]:
+                cp.start()
 
     def finish(t, u):
         g = add(part1, 1, t, u, 2)
         g1s[t, 24 * u:24 * (u + 1)] = g
         for k in range(2):
-            sb[2 * u + k, t] = g[12 * k:12 * (k + 1)]
-        if u == 1 and t < TASKS - 1:
-            send_back(t)
+            sb[2 * u + k, 12 * t:12 * (t + 1)] = g[12 * k:12 * (k + 1)]
         g2s[t, 24 * u:24 * (u + 1)] = add(part2, 2, t, u, 2)
 
     both = ((1, part1), (2, part2))
@@ -326,36 +355,44 @@
             go(part, i, *order[n], 1)
 
     slope(FROM_XZ, 1)
-    act(FROM_YZ, 1, 1)
     for t in range(TASKS):
         dz_of(FROM_XZ, 1, t, dzx)
         q_of(1, t, 1, dzx)
-        add_a(FROM_Z, t, 0)
+        if t:
+            add_a(FROM_Z, t, 0)
         add_a(FROM_XZ, t, 1)
         for u in range(2):
             go(part1, 1, t, u, 0)
+        if t:
+            first_hop(2 * t - 2)
+        if t == 0:
+            for cp in yz_x[2:]:
+                cp.wait_recv()
+            act(FROM_YZ, 1, 1)
         dz_of(FROM_YZ, 1, t, dz.at[1, t, 1])
         add_b(t, 0)
         add_b(t, 1)
         for u in range(2):
             go(part2, 2, t, u, 0)
         if t == 1:
-            first_hop(0)
             first_hop(1)
-    first_hop(2)
+    sb[:, 36:40, :] = jnp.zeros((4, 4, DIM), F32)
     for n in range(6):
         if n + 3 < 6:
             for i, part in both:
                 add(part, i, *order[n + 3], 0)
         for i, part in both:
-            cps[i, *order[n], 1].wait_recv()
+            arrived(i, *order[n], 1)
             if n + 3 < 6:
                 go(part, i, *order[n + 3], 1)
             merge(part, *order[n], 1)
             go(part, i, *order[n], 2)
-        if n >= 2:
+        if n >= 3:
             finish(*order[n - 2])
+    finish(*order[0])
+    send_back(0, inner)
     finish(*order[4])
+    send_back(0, outer)
     finish(*order[5])
 
     row = jnp.zeros((1, 128), F32)
@@ -365,7 +402,8 @@
         row = row + jnp.where(lane == i, jnp.sum(part, axis=1, keepdims=True), 0.0)
     grams[me] = row
     exchange_start(grams, ls.at[8], ls.at[9])
-    send_back(TASKS - 1)
+    for cp in back[3:]:
+        cp.start()
     rb[own] = sb[own]
     for t in range(TASKS):
         for k in range(3):
@@ -376,8 +414,8 @@
         parts = []
         for b in range(32):
             bzh, bzl, by, bx, bc = b >> 4, (b >> 3) & 1, (b >> 2) & 1, (b >> 1) & 1, b & 1
-            at0 = 192 * bc + 96 * bzl + 48 * by
-            parts.append(rb[2 * bzh + bx, t, :, at0:at0 + 48])
+            at0 = 192 * bc + 96 * (bzl ^ bzh) + 48 * by
+            parts.append(rb[2 * bzh + bx, 12 * t:12 * (t + 1), at0:at0 + 48])
         full = jnp.concatenate(parts, axis=1)
         for k in range(12):
             o1_ref[t, pl.ds(k, 12, stride=12), :] = full[:, 128 * k:128 * (k + 1)]
@@ -427,7 +465,7 @@
                 v((TASKS, 2, 48, DIM), F32), v((TASKS, 2, 48, DIM), F32),
                 v((TASKS, 2, 24, DIM), F32), v((TASKS, 2, 24, DIM), F32),
                 v((TASKS, 48, DIM), F32), v((TASKS, 48, DIM), F32),
-                v((4, TASKS, 12, DIM), F32), v((4, TASKS, 12, DIM), F32),
+                v((4, 40, DIM), F32), v((4, 40, DIM), F32),
                 dma((9,)), dma((N_SEM,)), dma((10,)),
             ],
             compiler_params=pltpu.CompilerParams(collective_id=0, has_side_effects=True, vmem_limit_bytes=28 * 2**20),

time: 60.9 us -> 59.7 us (0.980)
  Pallas kernels: 58.9 us -> 57.6 us
    pallas_call x1, Pallas kernels: 58.9 us -> 57.6 us  [step(): pl.pallas_call(kernel, name='step', out_shape=(jax.ShapeDtypeStruct((1, T...]
where the time goes in v4:
time: 59.7 us; the launch traced here: 59.5 us
  Pallas kernels  57.6 us (96%)
  other arithmetic  0.74 us (1%)
  between operations  0.64 us (1%)
    pallas_call x1, Pallas kernels, step(): pl.pallas_call(kernel, name='step', out_shape=(jax.ShapeDtypeStruct((1, T...  57.6 us

profile of v4, /device:TPU:0, one launch (start us, length us, event | category | flops | bytes accessed | tf_op | source)
XLA Modules:
  0.0 59.5 jit_solution(1573068205174155657)
XLA Ops:
  0.6 57.6 %step.1 = (f32[1,3]{1,0:T(1,128)S(1)}, f32[3,144,128]{2,1,0:T(8,128)S(1)}, f32[3,144,128]{2,1,0:T(8,128)S(1)}) custom-call(bf16[512,384]{1,0:T(8,128)(2,1)} %x_hbm.1, bf16[384,1536]{1,0:T(8,128)(2,1)} %w1_hbm.1, bf16[1536,384]{1,0:T(8,128)(2,1)} %w2_hbm.1, bf16[3,13,384]{2,1,0:T(8,128)(2,1)} %bitcast.8, s32[3,512]{1,0:T(4,128)} %lab_hbm.1, s32[3,512]{1,0:T(4,128)} %msk_hbm.1), custom_call_target="tpu_custom_call" | custom-call | tf_op jit(solution)/shard_map/step/pallas_call | solution.py:446
  58.3 0.7 %multiply_reduce_fusion = (f32[144,128]{1,0:T(8,128)}, f32[144,128]{1,0:T(8,128)}) fusion(f32[3,144,128]{2,1,0:T(8,128)S(1)} %get-tuple-element.8, f32[3]{0:T(128)S(1)} %bitcast.4, f32[3,144,128]{2,1,0:T(8,128)S(1)} %get-tuple-element.7), kind=kLoop, calls=%fused_computation | loop fusion | flops 184320 | bytes 589836 | tf_op jit(solution)/shard_map/reduce_sum | solution.py:476
  59.0 0.5 copy.10

commit v5 on v4

--- a/solution.py
+++ b/solution.py
@@ -12,7 +12,7 @@
 HALF = TOK // 2
 GELU_C = 0.7978845608028654
 GELU_A = 0.044715
-N_SEM = 68
+N_SEM = 66
 OWN, FROM_X, FROM_Z, FROM_XZ, FROM_Y, FROM_YZ = range(6)
 
 F32, BF16 = jnp.float32, jnp.bfloat16
@@ -24,6 +24,22 @@
 
 def dot_nt(a, b):
     return lax.dot_general(a, b, (((1,), (1,)), ((), ())), preferred_element_type=F32)
+
+
+def bit(v, i):
+    return (v >> i) & 1
+
+
+def flip(b):
+    return 1 - 2 * b
+
+
+def index(c, x, y, zl, zh):
+    return c + 2 * x + 4 * y + 8 * zl + 16 * zh
+
+
+def tile(k, n=128):
+    return slice(n * k, n * (k + 1))
 
 
 def gelu_cdf(p):
@@ -38,17 +54,11 @@
            rc1, rc2, ra1, ra2, rb1, rb2, g1s, g2s, sb, rb,
            ss, rs, ls):
     me = lax.axis_index("data")
-    c = lax.rem(me, 2)
-    x = lax.rem(me // 2, 2)
-    y = lax.rem(me // 4, 2)
-    zl = lax.rem(me // 8, 2)
-    zh = lax.rem(me // 16, 2)
-    to_c = me + (1 - 2 * c)
-    to_x = me + 2 * (1 - 2 * x)
-    to_y = me + 4 * (1 - 2 * y)
-    to_zl = me + 8 * (1 - 2 * zl)
-    to_zh = me + 16 * (1 - 2 * zh) + 8 * (1 - 2 * zl)
+    c, x, y, zl, zh = (lax.rem(me // n, 2) for n in (1, 2, 4, 8, 16))
+    to_c, to_x, to_y = me + flip(c), me + 2 * flip(x), me + 4 * flip(y)
+    to_zh = me + index(0, 0, 0, flip(zl), flip(zh))
     e = lax.rem(zh + zl, 2)
+    to_zl = me + 8 * flip(zl)
 
     used = []
 
@@ -92,12 +102,11 @@
 
     col = lax.broadcasted_iota(jnp.int32, (DIM, 1), 0)
     blk = (col * 43691) >> 19
-    dev = (((blk >> 3) & 1) + 4 * ((blk >> 2) & 1) + 8 * (((blk >> 1) ^ (blk >> 4)) & 1) + 16 * ((blk >> 4) & 1)
-           + 2 * (blk & 1))
+    dev = index(bit(blk, 3), bit(blk, 0), bit(blk, 2), bit(blk, 1) ^ bit(blk, 4), bit(blk, 4))
     perm = (lax.broadcasted_iota(jnp.int32, (DIM, DIM), 1) == 12 * dev + (col - 12 * blk)).astype(BF16)
     loads[0].wait()
     for h in range(2):
-        gx[OWN, h] = dot_nt(perm, x_ref[HALF * h:HALF * (h + 1), :]).astype(BF16)
+        gx[OWN, h] = dot_nt(perm, x_ref[tile(h, HALF), :]).astype(BF16)
     lane = lax.broadcasted_iota(jnp.int32, (1, 128), 1)
     row = jnp.zeros((1, 128), F32)
     loads[1].wait()
@@ -156,7 +165,7 @@
     cls = lax.broadcasted_iota(jnp.int32, (PAD, TOK), 0)
     valid = cls < CLS
     for t in range(TASKS):
-        lg = jnp.where(valid, logits[PAD * t:PAD * (t + 1)], -jnp.inf)
+        lg = jnp.where(valid, logits[tile(t, PAD)], -jnp.inf)
         ex = jnp.exp(lg - jnp.max(lg, axis=0, keepdims=True))
         sm = ex / jnp.sum(ex, axis=0, keepdims=True)
         hot = (lab_ref[t:t + 1, :] == cls).astype(F32)
@@ -170,21 +179,19 @@
 
     hid_iota = lax.broadcasted_iota(jnp.int32, (DIM, HID), 1)
     seg = (col * 43691) >> 21
-    src_a = 48 * ((seg >> 2) + 8 * (((seg >> 1) & 1) ^ zh) + 4 * (seg & 1) + 16 * zh + 2 * x) + (col - 48 * seg)
+    src_a = 48 * (index(bit(seg, 2), x, bit(seg, 0), bit(seg, 1) ^ zh, zh) - seg) + col
     seg = (col * 43691) >> 20
-    src_b = (48 * (((seg >> 2) & 1) + 2 * ((seg >> 1) & 1) + 8 * ((seg & 1) ^ zh) + 16 * zh + 4 * y)
-             + 24 * (seg >> 3) + (col - 24 * seg))
+    src_b = 48 * index(bit(seg, 2), bit(seg, 1), y, bit(seg, 0) ^ zh, zh) + 24 * (bit(seg, 3) - seg) + col
     for src, dst in ((src_a, w1a), (src_b, w1b)):
         sel = (hid_iota == src).astype(BF16)
         dst[...] = dot_nt(dot_nt(sel, w1_ref[...]).astype(BF16), perm).astype(BF16)
     for k in range(8):
-        eb = (k >> 1) & 1
-        dv = (k >> 2) + 8 * (eb + zh - 2 * eb * zh) + 4 * (k & 1) + 16 * zh + 2 * x
-        w2a[48 * k:48 * (k + 1), :] = w2_ref[pl.ds(pl.multiple_of(48 * dv, 16), 48), :]
-    for t in range(TASKS):
-        ht[t] = jnp.transpose(hp_ref[PAD * t:PAD * (t + 1), :].astype(F32)).astype(BF16)
-
-    strips = [slice(128 * r, 128 * (r + 1)) for r in range(3)]
+        dv = index(bit(k, 2), x, bit(k, 0), bit(k, 1) * flip(zh) + zh, zh)
+        w2a[tile(k, 48), :] = w2_ref[pl.ds(pl.multiple_of(48 * dv, 16), 48), :]
+    for t in range(TASKS):
+        ht[t] = jnp.transpose(hp_ref[tile(t, PAD), :].astype(F32)).astype(BF16)
+
+    strips = [tile(r) for r in range(TASKS)]
 
     def slope(s, h):
         for rows in strips:
@@ -198,7 +205,7 @@
             at[k, h, rows, :] = (p * gelu_cdf(p)[2]).astype(BF16)
 
     def dz_of(s, h, t, ref):
-        ref[...] = dot(ht[t], ge[s, t, :, HALF * h:HALF * (h + 1)]).astype(BF16)
+        ref[...] = dot(ht[t], ge[s, t, :, tile(h, HALF)]).astype(BF16)
 
     def q_of(h, t, k, ref):
         for rows in strips:
@@ -247,17 +254,17 @@
         add_b(t, 0, True)
     start_if(inner, z_x[4])
     start_if(outer, z_x[2])
+    start_if(outer, z_x[3])
     for cp in (x_e, x_x[0], x_x[1]):
         cp.wait_recv()
     forward(z_x[0], xz_x[0], yz_x[0])
     prep_a(FROM_X, 0, 0)
-    start_if(outer, z_x[3])
+    start_if(outer, z_x[4])
     forward(z_e, xz_e, yz_e)
     forward(z_x[1], xz_x[1], yz_x[1])
     prep_a(FROM_X, 1, 0)
     for t in range(TASKS):
         add_a(FROM_X, t, 0)
-    start_if(outer, z_x[4])
     for cp in (y_e, y_x[0], y_x[1]):
         cp.wait_recv()
     prep_b(FROM_Y, 0, 0)
@@ -283,21 +290,19 @@
         return pl.ds(pl.multiple_of(base, 8), n)
     bits1, bits2 = (c, y, e), (c, x, e)
     dest1, dest2 = (to_c, to_y, to_zl), (to_c, to_x, to_zl)
-    z_first = ((0, 0),)
-
-    def moves(bits, t, u, stage):
+
+    def moves(bits, u, stage):
+        bc, bm, be = bits
+
+        def pick(at0, b, n):
+            return at0 + n * (1 - b), at0 + n * b, n
         at0 = 192 * u
         if stage == 0:
-            return [(at0 + 96 * (1 - bits[0]), at0 + 96 * bits[0], 0, 96, 0)]
-        at0 = at0 + 96 * bits[0]
-        if (t, u) in z_first:
-            if stage == 1:
-                return [(at0 + 48 * b + 24 * (1 - bits[2]), at0 + 48 * b + 24 * bits[2], 24 * b, 24, 2) for b in range(2)]
-            return [(at0 + 48 * (1 - bits[1]) + 24 * bits[2], at0 + 48 * bits[1] + 24 * bits[2], 0, 24, 1)]
+            return pick(at0, bc, 96)
+        at0 = at0 + 96 * bc
         if stage == 1:
-            return [(at0 + 48 * (1 - bits[1]), at0 + 48 * bits[1], 0, 48, 1)]
-        at0 = at0 + 48 * bits[1]
-        return [(at0 + 24 * (1 - bits[2]), at0 + 24 * bits[2], 0, 24, 2)]
+            return pick(at0, bm, 48)
+        return pick(at0 + 48 * bm, be, 24)
 
     part1 = (acc1, (rc1, ra1, rb1), bits1, dest1)
     part2 = (acc2, (rc2, ra2, rb2), bits2, dest2)
@@ -306,28 +311,23 @@
 
     def go(part, i, t, u, stage):
         acc, recv, bits, dest = part
-        cps[i, t, u, stage] = [
-            start(rcopy(acc.at[t, rows(out, n)], recv[stage].at[t, u, pl.ds(at0, n)], dest[link], 2 * stage + i + 1))
-            for out, _, at0, n, link in moves(bits, t, u, stage)]
+        out, _, n = moves(bits, u, stage)
+        cps[i, t, u, stage] = start(
+            rcopy(acc.at[t, rows(out, n)], recv[stage].at[t, u], dest[stage], 2 * stage + i + 1))
 
     def merge(part, t, u, stage):
         acc, recv, bits, _ = part
-        for _, kept, at0, n, _ in moves(bits, t, u, stage):
-            mine = rows(kept, n)
-            v = acc[t, mine] + recv[stage][t, u, at0:at0 + n]
-            acc[t, mine] = v
+        _, kept, n = moves(bits, u, stage)
+        v = acc[t, rows(kept, n)] + recv[stage][t, u]
+        acc[t, rows(kept, n)] = v
         return v
 
-    def arrived(i, t, u, stage):
-        for cp in cps[i, t, u, stage]:
-            cp.wait_recv()
-
     def add(part, i, t, u, stage):
-        arrived(i, t, u, stage)
+        cps[i, t, u, stage].wait_recv()
         return merge(part, t, u, stage)
 
     own = 2 * zh + x
-    fx, fz = 1 - 2 * x, 2 * (1 - 2 * zh)
+    fx, fz = flip(x), 2 * flip(zh)
     back = []
 
     for part in (pl.ds(0, 24), pl.ds(24, 16)):
@@ -342,10 +342,10 @@
 
     def finish(t, u):
         g = add(part1, 1, t, u, 2)
-        g1s[t, 24 * u:24 * (u + 1)] = g
+        g1s[t, tile(u, 24)] = g
         for k in range(2):
-            sb[2 * u + k, 12 * t:12 * (t + 1)] = g[12 * k:12 * (k + 1)]
-        g2s[t, 24 * u:24 * (u + 1)] = add(part2, 2, t, u, 2)
+            sb[2 * u + k, tile(t, 12)] = g[tile(k, 12)]
+        g2s[t, tile(u, 24)] = add(part2, 2, t, u, 2)
 
     both = ((1, part1), (2, part2))
 
@@ -382,21 +382,20 @@
             for i, part in both:
                 add(part, i, *order[n + 3], 0)
         for i, part in both:
-            arrived(i, *order[n], 1)
+            cps[i, *order[n], 1].wait_recv()
             if n + 3 < 6:
                 go(part, i, *order[n + 3], 1)
             merge(part, *order[n], 1)
             go(part, i, *order[n], 2)
-        if n >= 3:
+        if n >= 2:
             finish(*order[n - 2])
-    finish(*order[0])
     send_back(0, inner)
     finish(*order[4])
     send_back(0, outer)
     finish(*order[5])
 
     row = jnp.zeros((1, 128), F32)
-    pairs = [(0, 0), (0, 1), (0, 2), (1, 1), (1, 2), (2, 2)]
+    pairs = [(t, s) for t in range(TASKS) for s in range(t, TASKS)]
     for i, (t, s) in enumerate(pairs):
         part = jnp.sum(g1s[t] * g1s[s] + g2s[t] * g2s[s], axis=0, keepdims=True)
         row = row + jnp.where(lane == i, jnp.sum(part, axis=1, keepdims=True), 0.0)
@@ -407,31 +406,31 @@
     rb[own] = sb[own]
     for t in range(TASKS):
         for k in range(3):
-            o2_ref[t, pl.ds(k, 48, stride=3), :] = g2s[t, :, 128 * k:128 * (k + 1)]
+            o2_ref[t, pl.ds(k, 48, stride=3), :] = g2s[t, :, tile(k)]
     for cp in back:
         cp.wait_recv()
     for t in range(TASKS):
         parts = []
         for b in range(32):
-            bzh, bzl, by, bx, bc = b >> 4, (b >> 3) & 1, (b >> 2) & 1, (b >> 1) & 1, b & 1
+            bc, bx, by, bzl, bzh = (bit(b, i) for i in range(5))
             at0 = 192 * bc + 96 * (bzl ^ bzh) + 48 * by
-            parts.append(rb[2 * bzh + bx, 12 * t:12 * (t + 1), at0:at0 + 48])
+            parts.append(rb[2 * bzh + bx, tile(t, 12), at0:at0 + 48])
         full = jnp.concatenate(parts, axis=1)
         for k in range(12):
-            o1_ref[t, pl.ds(k, 12, stride=12), :] = full[:, 128 * k:128 * (k + 1)]
+            o1_ref[t, pl.ds(k, 12, stride=12), :] = full[:, tile(k)]
     exchange_wait(grams, ls.at[9])
     m = jnp.sum(grams[...], axis=0)
     ent = [jnp.broadcast_to(m[:, i:i + 1], (8, 128)) for i in range(6)]
-    neg = -TASKS / (ent[0] + ent[3] + ent[5])
+    neg = -TASKS / sum(ent[i] for i, (t, s) in enumerate(pairs) if t == s)
     gram = {}
     for i, (t, s) in enumerate(pairs):
         gram[t, s] = gram[s, t] = ent[i] * neg
     w = [jnp.full((8, 128), 1.0 / TASKS, F32)] * TASKS
     for _ in range(SOLVER_STEPS):
-        up = [w[t] * jnp.exp(gram[t, 0] * w[0] + gram[t, 1] * w[1] + gram[t, 2] * w[2]) for t in range(TASKS)]
-        norm = 1.0 / (up[0] + up[1] + up[2])
+        up = [w[t] * jnp.exp(sum(gram[t, s] * w[s] for s in range(TASKS))) for t in range(TASKS)]
+        norm = 1.0 / sum(up)
         w = [v * norm for v in up]
-    al_ref[...] = jnp.where(lane == 0, w[0][:1], jnp.where(lane == 1, w[1][:1], w[2][:1]))[:, :TASKS]
+    al_ref[...] = sum(jnp.where(lane == t, w[t][:1], 0.0) for t in range(TASKS))[:, :TASKS]
     exchange_wait(cnts, ls.at[6])
     exchange_wait(grams, ls.at[8])
     for i, ref in enumerate((gx.at[pl.ds(0, 5)], ge.at[pl.ds(0, 5)], rc1, rc2, ra1, ra2, rb1, rb2, rb.at[pl.ds(0, 3)])):

time: 59.7 us -> 59.1 us (0.990)
  Pallas kernels: 57.6 us -> 57 us
where the time goes in v5:
time: 59.1 us; the launch traced here: 58.9 us
  Pallas kernels  57 us (96%)
  other arithmetic  0.74 us (1%)
  between operations  0.64 us (1%)
    pallas_call x1, Pallas kernels, step(): pl.pallas_call(kernel, name='step', out_shape=(jax.ShapeDtypeStruct((1, T...  57 us

profile of v5, /device:TPU:0, one launch (start us, length us, event | category | flops | bytes accessed | tf_op | source)
XLA Modules:
  0.0 58.9 jit_solution(407707864186651729)
XLA Ops:
  0.6 57.0 %step.1 = (f32[1,3]{1,0:T(1,128)S(1)}, f32[3,144,128]{2,1,0:T(8,128)S(1)}, f32[3,144,128]{2,1,0:T(8,128)S(1)}) custom-call(bf16[512,384]{1,0:T(8,128)(2,1)} %x_hbm.1, bf16[384,1536]{1,0:T(8,128)(2,1)} %w1_hbm.1, bf16[1536,384]{1,0:T(8,128)(2,1)} %w2_hbm.1, bf16[3,13,384]{2,1,0:T(8,128)(2,1)} %bitcast.8, s32[3,512]{1,0:T(4,128)} %lab_hbm.1, s32[3,512]{1,0:T(4,128)} %msk_hbm.1), custom_call_target="tpu_custom_call" | custom-call | tf_op jit(solution)/shard_map/step/pallas_call | solution.py:445
  57.7 0.7 %multiply_reduce_fusion = (f32[144,128]{1,0:T(8,128)}, f32[144,128]{1,0:T(8,128)}) fusion(f32[3,144,128]{2,1,0:T(8,128)S(1)} %get-tuple-element.8, f32[3]{0:T(128)S(1)} %bitcast.4, f32[3,144,128]{2,1,0:T(8,128)S(1)} %get-tuple-element.7), kind=kLoop, calls=%fused_computation | loop fusion | flops 184320 | bytes 589836 | tf_op jit(solution)/shard_map/reduce_sum | solution.py:475
  58.4 0.5 copy.10

commit v6 on v5

--- a/solution.py
+++ b/solution.py
@@ -118,7 +118,7 @@
 
     def piece(slot, h, r0=0, n=DIM):
         return gx.at[slot, h, pl.ds(r0, n)]
-    cuts = ((0, 0, 192), (0, 192, 192), (1, 0, 192), (1, 192, 128), (1, 320, 64))
+    cuts = ((0, 0, 192), (0, 192, 192), (1, 0, 192), (1, 192, 96), (1, 288, 96))
     z_x = [rcopy(piece(OWN, *k), piece(FROM_Z, *k), to_zh, 0) for k in cuts]
     x_x = [rcopy(piece(OWN, h), piece(FROM_X, h), to_x, 0) for h in range(2)]
     y_x = [rcopy(piece(OWN, h), piece(FROM_Y, h), to_y, 0) for h in range(2)]

time: 59.1 us -> 59 us (level)
  no operation moved by 1% of the time
where the time goes in v6:
time: 59 us; the launch traced here: 58.9 us
  Pallas kernels  57 us (97%)
  other arithmetic  0.74 us (1%)
  between operations  0.64 us (1%)
    pallas_call x1, Pallas kernels, step(): pl.pallas_call(kernel, name='step', out_shape=(jax.ShapeDtypeStruct((1, T...  57 us

profile of v6, /device:TPU:0, one launch (start us, length us, event | category | flops | bytes accessed | tf_op | source)
XLA Modules:
  0.0 58.9 jit_solution(10243032694909407226)
XLA Ops:
  0.6 57.0 %step.1 = (f32[1,3]{1,0:T(1,128)S(1)}, f32[3,144,128]{2,1,0:T(8,128)S(1)}, f32[3,144,128]{2,1,0:T(8,128)S(1)}) custom-call(bf16[512,384]{1,0:T(8,128)(2,1)} %x_hbm.1, bf16[384,1536]{1,0:T(8,128)(2,1)} %w1_hbm.1, bf16[1536,384]{1,0:T(8,128)(2,1)} %w2_hbm.1, bf16[3,13,384]{2,1,0:T(8,128)(2,1)} %bitcast.8, s32[3,512]{1,0:T(4,128)} %lab_hbm.1, s32[3,512]{1,0:T(4,128)} %msk_hbm.1), custom_call_target="tpu_custom_call" | custom-call | tf_op jit(solution)/shard_map/step/pallas_call | solution.py:445
  57.6 0.7 %multiply_reduce_fusion = (f32[144,128]{1,0:T(8,128)}, f32[144,128]{1,0:T(8,128)}) fusion(f32[3,144,128]{2,1,0:T(8,128)S(1)} %get-tuple-element.8, f32[3]{0:T(128)S(1)} %bitcast.4, f32[3,144,128]{2,1,0:T(8,128)S(1)} %get-tuple-element.7), kind=kLoop, calls=%fused_computation | loop fusion | flops 184320 | bytes 589836 | tf_op jit(solution)/shard_map/reduce_sum | solution.py:475
  58.3 0.5 copy.10

commit v7 on v6

--- a/solution.py
+++ b/solution.py
@@ -83,7 +83,7 @@
         def go(i, _):
             row_copy(buf, me, s_sem, r_sem, lax.rem(me + i, N_DEV)).start()
             return 0
-        lax.fori_loop(1, N_DEV, go, 0)
+        lax.fori_loop(1, N_DEV, go, 0, unroll=True)
 
     def exchange_wait(buf, sem):
         wait_bytes(buf.at[pl.ds(0, N_DEV - 1)], sem)

time: 59 us -> 59 us (level)
  no operation moved by 1% of the time
where the time goes in v7:
time: 59 us; the launch traced here: 58.9 us
  Pallas kernels  57 us (97%)
  other arithmetic  0.74 us (1%)
  between operations  0.64 us (1%)
    pallas_call x1, Pallas kernels, step(): pl.pallas_call(kernel, name='step', out_shape=(jax.ShapeDtypeStruct((1, T...  57 us

profile of v7, /device:TPU:0, one launch (start us, length us, event | category | flops | bytes accessed | tf_op | source)
XLA Modules:
  0.0 58.9 jit_solution(7974508408275614881)
XLA Ops:
  0.6 57.0 %step.1 = (f32[1,3]{1,0:T(1,128)S(1)}, f32[3,144,128]{2,1,0:T(8,128)S(1)}, f32[3,144,128]{2,1,0:T(8,128)S(1)}) custom-call(bf16[512,384]{1,0:T(8,128)(2,1)} %x_hbm.1, bf16[384,1536]{1,0:T(8,128)(2,1)} %w1_hbm.1, bf16[1536,384]{1,0:T(8,128)(2,1)} %w2_hbm.1, bf16[3,13,384]{2,1,0:T(8,128)(2,1)} %bitcast.8, s32[3,512]{1,0:T(4,128)} %lab_hbm.1, s32[3,512]{1,0:T(4,128)} %msk_hbm.1), custom_call_target="tpu_custom_call" | custom-call | tf_op jit(solution)/shard_map/step/pallas_call | solution.py:445
  57.6 0.7 %multiply_reduce_fusion = (f32[144,128]{1,0:T(8,128)}, f32[144,128]{1,0:T(8,128)}) fusion(f32[3,144,128]{2,1,0:T(8,128)S(1)} %get-tuple-element.8, f32[3]{0:T(128)S(1)} %bitcast.4, f32[3,144,128]{2,1,0:T(8,128)S(1)} %get-tuple-element.7), kind=kLoop, calls=%fused_computation | loop fusion | flops 184320 | bytes 589836 | tf_op jit(solution)/shard_map/reduce_sum | solution.py:475
  58.3 0.5 copy.10
